TPU v7x, 256 devices: a whole 4x4x8 slice. The times are simulated.
256 devices in a mesh: seq: 16 (over x, z_lo), row: 2 (over core), col: 8 (over z_hi, y).
Axes of the slice: x: 4, y: 4, z: 8 (z_hi: 2, z_lo: 4; z = z_hi * 4 + z_lo), core: 2. Of those that a mesh axis runs over, the one named last changes fastest.
Arguments:
- tokens: bfloat16 [8192, 6144], P('seq', ('row', 'col')), may hold values from -20 to 20
- ln_gain: bfloat16 [6144], P(('row', 'col')), may hold values from 0.099609375 to 1.8984375
- ln_bias: bfloat16 [6144], P(('row', 'col')), may hold values from -1.5 to 1.5
- w_qkv: bfloat16 [3, 6144, 4096], P(None, 'row', 'col'), may hold values from -3 to 3
- w_out: bfloat16 [4096, 6144], P('col', 'row'), may hold values from -0.5 to 0.5
Outputs:
- attended: bfloat16 [8192, 6144], P('seq', ('row', 'col'))
All inputs are finite; a program needn't handle non-finite values.
Results may differ from a plain program's by a relative error of at most 0.014.
Values may be sent and summed in bfloat16 or wider, within the bound.
A program may use at most 128 MiB of HBM per device.

v0:
```python
import math

import jax
import jax.numpy as jnp
from jax import lax
from jax.sharding import Mesh
from jax.sharding import PartitionSpec as P

D = 6144
HD = 128
ROW_COL = ("row", "col_0", "col_1")
COL = ("col_0", "col_1")


EPS = 0.25


def side_by_side(arrays, axis, dim, along):
    both = jnp.concatenate(arrays, axis=along)
    result, at, finished = (lax.all_gather(both, axis, axis=dim, tiled=True), 0, [])
    for a in arrays:
        finished.append(lax.slice_in_dim(result, at, at + a.shape[along], axis=along))
        at += a.shape[along]
    return tuple(finished)


def split_up(value, dim, length):
    before, after = (value.shape[:dim], value.shape[dim + 1 :])
    return jnp.moveaxis(value.reshape(*before, length, -1, *after), dim, 0)


def sent_and_summed(value, axis, dim):
    tiles = split_up(value, dim, lax.axis_size(axis))
    arrived = lax.all_to_all(tiles, axis, split_axis=0, concat_axis=0, tiled=True)
    return arrived.sum(axis=0)


def sent_to_all(value, axis):
    length = lax.axis_size(axis)
    return lax.all_to_all(
        jnp.broadcast_to(value[None], (length, *value.shape)), axis, 0, 0, tiled=True
    )


def laid_out(tiles, dim):
    tiles = jnp.moveaxis(tiles, 0, dim)
    dims = tiles.shape
    return tiles.reshape(*dims[:dim], dims[dim] * dims[dim + 1], *dims[dim + 2 :])


def gather_directly(value, axis, dim):
    tiles = sent_to_all(value, axis)
    return laid_out(tiles, dim)


def reduced_to_own(tiles, axes, order):
    dims = [lax.axis_size(a) for a in axes]
    tiles = tiles.reshape(*dims, *tiles.shape[1:])
    tiles = tiles.transpose(*order, *range(len(axes), tiles.ndim))
    tiles = tiles.reshape(-1, *tiles.shape[len(axes) :])
    for k in order:
        tiles = lax.psum_scatter(tiles, axes[k], scatter_dimension=0, tiled=True)
    return tiles[0]


def sum_by_axis(value, axes, order, dim):
    length = lax.axis_size(axes)
    return reduced_to_own(split_up(value, dim, length), axes, order)


def block_length(row_total):
    block_size = row_total
    while block_size > 2048 and block_size % 2 == 0:
        block_size = block_size // 2
    return block_size


def initial_state(head_count, query_count):
    return (
        jnp.full((head_count, query_count), -1e30, jnp.float32),
        jnp.zeros((head_count, query_count), jnp.float32),
        jnp.zeros((head_count, query_count, HD), jnp.float32),
    )


def attend(carried, queries, key_rows, value_rows):
    score_scale = 1.0 / math.sqrt(HD)
    key_axis = 0
    row_total = key_rows.shape[key_axis]
    block_size = block_length(row_total)
    block_count = row_total // block_size
    key_form = "khd"

    def fold_block(running, block_index):
        running_max, running_sum, weighted = running
        first = block_index * block_size
        key_block = lax.dynamic_slice_in_dim(key_rows, first, block_size, key_axis)
        value_block = lax.dynamic_slice_in_dim(value_rows, first, block_size, key_axis)
        scores = (
            jnp.einsum(
                "hqd," + key_form + "->hqk", queries, key_block, preferred_element_type=jnp.float32
            )
            * score_scale
        )
        new_max = jnp.maximum(running_max, jnp.max(scores, axis=2))
        shrink = jnp.exp(running_max - new_max)
        weights = jnp.exp(scores - new_max[:, :, None])
        running_sum = running_sum * shrink + jnp.sum(weights, axis=2)
        weighted = weighted * shrink[:, :, None] + jnp.einsum(
            "hqk," + key_form + "->hqd",
            weights.astype(jnp.bfloat16),
            value_block,
            preferred_element_type=jnp.float32,
        )
        return ((new_max, running_sum, weighted), None)

    folded, _ = lax.scan(fold_block, carried, jnp.arange(block_count, dtype=jnp.int32))
    return folded


def normalize_heads(folded):
    return (folded[2] / folded[1][:, :, None]).astype(jnp.bfloat16)


def flatten_heads(per_head):
    return jnp.transpose(per_head, (1, 0, 2)).reshape(per_head.shape[1], per_head.shape[0] * HD)


def body(tokens, ln_gain, ln_bias, w_qkv, w_out):
    seq_rows = tokens.shape[0]
    gain_row = ln_gain[None, :]
    bias_row = ln_bias[None, :]
    whole_tok, whole_gain, whole_bias = side_by_side((tokens, gain_row, bias_row), ROW_COL, 1, 0)
    whole_float = whole_tok.astype(jnp.float32)
    feature_sum = jnp.sum(whole_float, axis=1)
    squares = jnp.sum(whole_float * whole_float, axis=1)
    half_width = whole_tok.shape[1] // lax.axis_size("row")
    offset = lax.axis_index("row") * half_width
    as_float = lax.dynamic_slice_in_dim(whole_float, offset, half_width, 1)
    half_gain = lax.dynamic_slice_in_dim(whole_gain, offset, half_width, 1)
    half_bias = lax.dynamic_slice_in_dim(whole_bias, offset, half_width, 1)
    token_mean = feature_sum / D
    spread = squares / D - token_mean * token_mean
    normed = (
        (as_float - token_mean[:, None])
        * lax.rsqrt(spread + EPS)[:, None]
        * half_gain.astype(jnp.float32)
        + half_bias.astype(jnp.float32)
    ).astype(jnp.bfloat16)
    row_share = seq_rows // lax.axis_size("row")
    local_heads = w_qkv.shape[2] // HD
    projected = sent_and_summed(
        jnp.einsum("td,kdn->tkn", normed, w_qkv, preferred_element_type=jnp.float32), "row", 0
    ).astype(jnp.bfloat16)
    queries = jnp.transpose(projected[:, 0].reshape(row_share, local_heads, HD), (1, 0, 2))
    shard_piece = side_by_side((projected[:, 1], projected[:, 2]), ("seq", "row"), 0, 1)
    pieces_k = shard_piece[0].reshape(shard_piece[0].shape[0], local_heads, HD)
    pieces_v = shard_piece[1].reshape(shard_piece[1].shape[0], local_heads, HD)
    folded = attend(initial_state(local_heads, row_share), queries, pieces_k, pieces_v)
    context = flatten_heads(normalize_heads(folded))
    partial_output = jnp.dot(
        gather_directly(context, "row", 0), w_out, preferred_element_type=jnp.float32
    )
    summed_output = sum_by_axis(partial_output.astype(jnp.bfloat16), COL, (1, 0), 1).astype(
        jnp.float32
    )
    return (tokens.astype(jnp.float32) + summed_output).astype(jnp.bfloat16)


def solution(mesh):
    finer = Mesh(
        mesh.devices.reshape(mesh.shape["seq"], mesh.shape["row"], 2, 4),
        ("seq", "row", "col_0", "col_1"),
    )
    in_specs = (P("seq", ROW_COL), P(ROW_COL), P(ROW_COL), P(None, "row", COL), P(COL, "row"))
    out_specs = P("seq", ROW_COL)
    return jax.shard_map(body, mesh=finer, in_specs=in_specs, out_specs=out_specs, check_vma=False)
```

profile of v0, /device:TPU:1, one launch (start us, length us, event | category | flops | bytes accessed | tf_op | source)
XLA Modules:
  0.0 454.5 jit_solution(6702434570306077203)
XLA Ops:
  10.1 100.0 %all-gather.3.cloned.1.call-done = bf16[514,6144]{1,0:T(8,128)(2,1)} async-done(((bf16[514,384]{1,0:T(8,128)(2,1)}), bf16[514,6144]{1,0:T(8,128)(2,1)}) %all-gather.3.cloned.1.call-update) | async-done | bytes 6316048 | tf_op jit(solution)/shard_map/all_gather | solution.py:20
  110.0 5.0 %fusion.19 = (f32[512]{0:T(512)S(1)}, f32[512]{0:T(512)S(1)}) fusion(bf16[514,6144]{1,0:T(8,128)(2,1)} %all-gather.3.cloned.1.call-done), kind=kLoop, calls=%fused_computation.23 | loop fusion | flops 12581888 | bytes 6295552 | tf_op jit(solution)/shard_map/reduce_sum | solution.py:135
  116.1 6.2 %slice_convert_fusion = f32[512,6144]{1,0:T(8,128)} fusion(bf16[514,6144]{1,0:T(8,128)(2,1)S(1)} %copy-done.2), kind=kLoop, calls=%fused_computation.21 | loop fusion | flops 3145728 | bytes 18874368 | tf_op jit(solution)/shard_map/convert_element_type | solution.py:134
  122.3 7.3 %fusion.21 = f32[512,3,512]{2,0,1:T(8,128)S(1)} fusion(bf16[3,3072,512]{2,1,0:T(8,128)(2,1)S(1)} %bitcast.70, f32[512,6144]{1,0:T(8,128)} %slice_convert_fusion, s32[]{:T(128)S(6)} %select_n.4, f32[3072]{0:T(1024)S(1)} %bitcast.67, f32[3072]{0:T(1024)S(1)} %bitcast.68, f32[512]{0:T(512)S(1)} %get-tuple-element.123, f32[512]{0:T(512)S(1)} %get-tuple-element.122), kind=kOutput, calls=%fused_computation.26 | convolution fusion | flops 4839702528 | bytes 18903044 | tf_op jit(solution)/shard_map/td,kdn->tkn/dot_general | solution.py:153
  130.2 7.1 %all_to_all.10 = f32[2,256,3,512]{3,1,2,0:T(8,128)} all-to-all(f32[2,256,3,512]{3,1,2,0:T(8,128)S(1)} %copy.20), channel_id=1, replica_groups=mesh['seq'=16,'row'=2,'col_0'=2,'col_1'=4] {'row'}, dimensions={0} | all-to-all | bytes 6291456 | tf_op jit(solution)/shard_map/all_to_all | solution.py:34
  145.0 93.2 %all-gather.5.cloned.1.call-done = bf16[8192,1024]{1,0:T(8,128)(2,1)} async-done(((bf16[256,1024]{1,0:T(8,128)(2,1)}), bf16[8192,1024]{1,0:T(8,128)(2,1)}) %all-gather.5.cloned.1.call-update) | async-done | bytes 16777232 | tf_op jit(solution)/shard_map/all_gather | solution.py:20
  238.2 11.3 %fusion.29 = (bf16[8192,512]{1,0:T(8,128)(2,1)}, bf16[8192,512]{1,0:T(8,128)(2,1)}) fusion(bf16[8192,1024]{1,0:T(8,128)(2,1)} %all-gather.5.cloned.1.call-done), kind=kLoop, calls=%fused_computation.43 | loop fusion | bytes 33554432 | tf_op jit(solution)/shard_map/slice | solution.py:22
  249.5 12.0 %copy.21 = bf16[8192,512]{0,1:T(8,128)(2,1)} copy(bf16[8192,512]{1,0:T(8,128)(2,1)} %get-tuple-element.116) | data formatting | bytes 16777216 | tf_op jit(solution)/shard_map/slice | solution.py:22
  261.5 12.0 %copy.23 = bf16[8192,512]{0,1:T(8,128)(2,1)} copy(bf16[8192,512]{1,0:T(8,128)(2,1)} %get-tuple-element.115) | data formatting | bytes 16777216 | tf_op jit(solution)/shard_map/slice | solution.py:22
  273.4 70.8 %while.15 = (s32[]{:T(128)}, f32[4,256]{1,0:T(4,128)S(1)}, f32[4,256]{1,0:T(4,128)S(1)}, f32[4,256,128]{2,1,0:T(8,128)}, s32[4]{0:T(128)S(1)}, /*index=5*/bf16[8...) while((s32[]{:T(128)}, f32[4,256]{1,0:T(4,128)S(1)}, ...), condition=%wide.region_6.7_spmd.clone, body=%wide.region_3.6_spmd.clone.sunk | while | flops 1090917376 | bytes 64291036 | solution.py:117
  274.7 6.1 %bitcast_reduce_fusion.2 = (f32[4,256]{1,0:T(4,128)S(1)}, f32[4,2048,256]{2,1,0:T(8,128)}) fusion(bf16[4,256,128]{2,1,0:T(8,128)(2,1)S(1)} %get-tuple-element.213, bf16[8192,4,128]{0,2,1:T(8,128)(2,1)} %get-tuple-element.212, s32[]{:T(128)S(6)} %select_n.12), kind=kOutput, calls=%fused_computation.1.clone.1 | convolution fusion | flops 541064192 | bytes 10752004 | tf_op jit(solution)/shard_map/while/body/eval_jaxpr/hqd,khd->hqk/dot_general | solution.py:100
  280.8 4.9 %fusion.45 = f32[4,256]{1,0:T(4,128)S(1)} fusion(f32[4,2048,256]{2,1,0:T(8,128)} %get-tuple-element.180, f32[4,256]{1,0:T(4,128)S(1)} %select_maximum_fusion.2), kind=kLoop, calls=%fused_computation.4.clone.1 | loop fusion | flops 6290432 | bytes 8396800 | tf_op jit(solution)/shard_map/while/body/eval_jaxpr/reduce_sum | solution.py:108
  292.3 6.1 %bitcast_reduce_fusion.2 = (f32[4,256]{1,0:T(4,128)S(1)}, f32[4,2048,256]{2,1,0:T(8,128)}) fusion(bf16[4,256,128]{2,1,0:T(8,128)(2,1)S(1)} %get-tuple-element.213, bf16[8192,4,128]{0,2,1:T(8,128)(2,1)} %get-tuple-element.212, s32[]{:T(128)S(6)} %select_n.12), kind=kOutput, calls=%fused_computation.1.clone.1 | convolution fusion | flops 541064192 | bytes 10752004 | tf_op jit(solution)/shard_map/while/body/eval_jaxpr/hqd,khd->hqk/dot_general | solution.py:100
  298.5 4.9 %fusion.45 = f32[4,256]{1,0:T(4,128)S(1)} fusion(f32[4,2048,256]{2,1,0:T(8,128)} %get-tuple-element.180, f32[4,256]{1,0:T(4,128)S(1)} %select_maximum_fusion.2), kind=kLoop, calls=%fused_computation.4.clone.1 | loop fusion | flops 6290432 | bytes 8396800 | tf_op jit(solution)/shard_map/while/body/eval_jaxpr/reduce_sum | solution.py:108
  304.2 4.6 %fusion.47 = f32[4,256,128]{2,1,0:T(8,128)} fusion(bf16[8192,4,128]{0,2,1:T(8,128)(2,1)} %get-tuple-element.214, s32[]{:T(128)S(6)} %select_n.12, f32[4,2048,256]{2,1,0:T(8,128)S(1)} %copy-done.1, f32[4,256]{1,0:T(4,128)S(1)} %select_maximum_fusion.2, f32[4,256,128]{2,1,0:T(8,128)} %get-tuple-element.198, f32[4,256]{1,0:T(4,128)S(1)} %get-tuple-element.182, ...), kind=kOutput, calls=%fused_computation.11.clone.1 | convolution fusion | flops 543555584 | bytes 11542533 | tf_op jit(solution)/shard_map/while/body/eval_jaxpr/hqk,khd->hqd/dot_general | solution.py:109
  310.1 6.1 %bitcast_reduce_fusion.2 = (f32[4,256]{1,0:T(4,128)S(1)}, f32[4,2048,256]{2,1,0:T(8,128)}) fusion(bf16[4,256,128]{2,1,0:T(8,128)(2,1)S(1)} %get-tuple-element.213, bf16[8192,4,128]{0,2,1:T(8,128)(2,1)} %get-tuple-element.212, s32[]{:T(128)S(6)} %select_n.12), kind=kOutput, calls=%fused_computation.1.clone.1 | convolution fusion | flops 541064192 | bytes 10752004 | tf_op jit(solution)/shard_map/while/body/eval_jaxpr/hqd,khd->hqk/dot_general | solution.py:100
  316.2 4.9 %fusion.45 = f32[4,256]{1,0:T(4,128)S(1)} fusion(f32[4,2048,256]{2,1,0:T(8,128)} %get-tuple-element.180, f32[4,256]{1,0:T(4,128)S(1)} %select_maximum_fusion.2), kind=kLoop, calls=%fused_computation.4.clone.1 | loop fusion | flops 6290432 | bytes 8396800 | tf_op jit(solution)/shard_map/while/body/eval_jaxpr/reduce_sum | solution.py:108
  322.0 4.6 %fusion.47 = f32[4,256,128]{2,1,0:T(8,128)} fusion(bf16[8192,4,128]{0,2,1:T(8,128)(2,1)} %get-tuple-element.214, s32[]{:T(128)S(6)} %select_n.12, f32[4,2048,256]{2,1,0:T(8,128)S(1)} %copy-done.1, f32[4,256]{1,0:T(4,128)S(1)} %select_maximum_fusion.2, f32[4,256,128]{2,1,0:T(8,128)} %get-tuple-element.198, f32[4,256]{1,0:T(4,128)S(1)} %get-tuple-element.182, ...), kind=kOutput, calls=%fused_computation.11.clone.1 | convolution fusion | flops 543555584 | bytes 11542533 | tf_op jit(solution)/shard_map/while/body/eval_jaxpr/hqk,khd->hqd/dot_general | solution.py:109
  327.8 6.1 %bitcast_reduce_fusion.2 = (f32[4,256]{1,0:T(4,128)S(1)}, f32[4,2048,256]{2,1,0:T(8,128)}) fusion(bf16[4,256,128]{2,1,0:T(8,128)(2,1)S(1)} %get-tuple-element.213, bf16[8192,4,128]{0,2,1:T(8,128)(2,1)} %get-tuple-element.212, s32[]{:T(128)S(6)} %select_n.12), kind=kOutput, calls=%fused_computation.1.clone.1 | convolution fusion | flops 541064192 | bytes 10752004 | tf_op jit(solution)/shard_map/while/body/eval_jaxpr/hqd,khd->hqk/dot_general | solution.py:100
  333.9 4.9 %fusion.45 = f32[4,256]{1,0:T(4,128)S(1)} fusion(f32[4,2048,256]{2,1,0:T(8,128)} %get-tuple-element.180, f32[4,256]{1,0:T(4,128)S(1)} %select_maximum_fusion.2), kind=kLoop, calls=%fused_computation.4.clone.1 | loop fusion | flops 6290432 | bytes 8396800 | tf_op jit(solution)/shard_map/while/body/eval_jaxpr/reduce_sum | solution.py:108
  339.7 4.6 %fusion.47 = f32[4,256,128]{2,1,0:T(8,128)} fusion(bf16[8192,4,128]{0,2,1:T(8,128)(2,1)} %get-tuple-element.214, s32[]{:T(128)S(6)} %select_n.12, f32[4,2048,256]{2,1,0:T(8,128)S(1)} %copy-done.1, f32[4,256]{1,0:T(4,128)S(1)} %select_maximum_fusion.2, f32[4,256,128]{2,1,0:T(8,128)} %get-tuple-element.198, f32[4,256]{1,0:T(4,128)S(1)} %get-tuple-element.182, ...), kind=kOutput, calls=%fused_computation.11.clone.1 | convolution fusion | flops 543555584 | bytes 11542533 | tf_op jit(solution)/shard_map/while/body/eval_jaxpr/hqk,khd->hqd/dot_general | solution.py:109
  357.6 6.2 %reshape.46 = bf16[2,4,512,384]{3,1,0,2:T(4,128)(2,1)} reshape(bf16[8,512,384]{2,0,1:T(8,128)(2,1)} %bitcast.61) | data formatting | bytes 6291456 | tf_op jit(solution)/shard_map/reshape | solution.py:58
  367.9 41.4 %reduce-scatter.3.cloned.1.call-done = bf16[2,512,384]{2,1,0:T(8,128)(2,1)} async-done(((bf16[8,512,384]{2,1,0:T(8,128)(2,1)}), bf16[2,512,384]{2,1,0:T(8,128)(2,1)}) %reduce-scatter.3.cloned.1.call-update) | async-done | bytes 786448 | tf_op jit(solution)/shard_map/reduce_scatter | solution.py:62
  409.3 36.8 %reduce-scatter.5.cloned.1.call-done = bf16[1,512,384]{2,1,0:T(8,128)(2,1)} async-done(((bf16[2,512,384]{2,1,0:T(8,128)(2,1)}), bf16[1,512,384]{2,1,0:T(8,128)(2,1)}) %reduce-scatter.5.cloned.1.call-update) | async-done | bytes 393232 | tf_op jit(solution)/shard_map/reduce_scatter | solution.py:62
  (71 shorter events, 42.2 us)
Async XLA Ops:
  6.5 346.8 %copy-start = (bf16[512,3072]{1,0:T(8,128)(2,1)S(1)}, bf16[512,3072]{1,0:T(8,128)(2,1)}, u32[]{:S(2)}) copy-start(bf16[512,3072]{1,0:T(8,128)(2,1)} %param.11) | copy-start | bytes 9437188
  6.5 103.5 %all-gather.3.cloned.1.call-start = ((), (), s32[]{:S(2)}) async-start(), calls=%async_computation.4 | async-start | bytes 6789120 | tf_op jit(solution)/shard_map/all_gather | solution.py:20
  10.0 228.2 %all-gather.5.cloned.1.call-start = ((), (), s32[]{:S(2)}) async-start(), calls=%async_computation.5 | async-start | bytes 17301504 | tf_op jit(solution)/shard_map/all_gather | solution.py:20
  110.0 6.1 %copy-start.2 = (bf16[514,6144]{1,0:T(8,128)(2,1)S(1)}, bf16[514,6144]{1,0:T(8,128)(2,1)}, u32[]{:S(2)}) copy-start(bf16[514,6144]{1,0:T(8,128)(2,1)} %all-gather.3.cloned.1.call-done) | copy-start | bytes 18948100
  110.0 12.3 %slice-start = ((s8[9437184]{0:T(1024)(128)(4,1)}), s8[4194304]{0:T(1024)(128)(4,1)S(1)}, s32[]{:S(2)}) async-start(s8[9437184]{0:T(1024)(128)(4,1)} %bitcast.69), calls=%async_computation.8 | async-start | bytes 8388608
  116.1 6.2 %slice-start.1 = ((s8[9437184]{0:T(1024)(128)(4,1)}), s8[4194304]{0:T(1024)(128)(4,1)S(1)}, s32[]{:S(2)}) async-start(s8[9437184]{0:T(1024)(128)(4,1)} %bitcast.69), calls=%async_computation.9 | async-start | bytes 8388608
  116.1 6.2 %slice-start.2 = ((s8[9437184]{0:T(1024)(128)(4,1)}), s8[1048576]{0:T(1024)(128)(4,1)S(1)}, s32[]{:S(2)}) async-start(s8[9437184]{0:T(1024)(128)(4,1)} %bitcast.69), calls=%async_computation.10 | async-start | bytes 2097152
  142.7 266.6 %reduce-scatter.3.cloned.1.call-start = ((), (), s32[]{:S(2)}) async-start(), calls=%async_computation.6 | async-start | bytes 3932160 | tf_op jit(solution)/shard_map/reduce_scatter | solution.py:62
  280.8 5.8 %copy-start.1 = (f32[4,2048,256]{2,1,0:T(8,128)S(1)}, f32[4,2048,256]{2,1,0:T(8,128)}, u32[]{:S(2)}) copy-start(f32[4,2048,256]{2,1,0:T(8,128)} %get-tuple-element.180) | copy-start | bytes 25165828 | tf_op jit(solution)/shard_map/while
  298.5 5.8 %copy-start.1 = (f32[4,2048,256]{2,1,0:T(8,128)S(1)}, f32[4,2048,256]{2,1,0:T(8,128)}, u32[]{:S(2)}) copy-start(f32[4,2048,256]{2,1,0:T(8,128)} %get-tuple-element.180) | copy-start | bytes 25165828 | tf_op jit(solution)/shard_map/while
  316.2 5.8 %copy-start.1 = (f32[4,2048,256]{2,1,0:T(8,128)S(1)}, f32[4,2048,256]{2,1,0:T(8,128)}, u32[]{:S(2)}) copy-start(f32[4,2048,256]{2,1,0:T(8,128)} %get-tuple-element.180) | copy-start | bytes 25165828 | tf_op jit(solution)/shard_map/while
  333.9 5.8 %copy-start.1 = (f32[4,2048,256]{2,1,0:T(8,128)S(1)}, f32[4,2048,256]{2,1,0:T(8,128)}, u32[]{:S(2)}) copy-start(f32[4,2048,256]{2,1,0:T(8,128)} %get-tuple-element.180) | copy-start | bytes 25165828 | tf_op jit(solution)/shard_map/while
  357.6 88.5 %copy-start.3 = (bf16[512,384]{1,0:T(8,128)(2,1)S(1)}, bf16[512,384]{1,0:T(8,128)(2,1)}, u32[]{:S(2)}) copy-start(bf16[512,384]{1,0:T(8,128)(2,1)} %param.7) | copy-start | bytes 1179652
  367.8 78.3 %reduce-scatter.5.cloned.1.call-start = ((), (), s32[]{:S(2)}) async-start(), calls=%async_computation.7 | async-start | bytes 1179648 | tf_op jit(solution)/shard_map/reduce_scatter | solution.py:62
Sparse Core Ops, SparseCore 0:
  10.1 99.8 all-gather.2
  142.8 95.2 all-gather.4
  367.9 41.3 reduce-scatter.2
  411.7 34.3 reduce-scatter.4
where the time goes:
time: 456 us; the launch traced here: 454 us
  waiting for transfers between devices  271 us (59%)
  local copies, waits for them, and re-layouts  63.8 us (14%)
  matrix products  52 us (11%)
  other arithmetic  39.9 us (9%)
  between operations  13.2 us (3%)
  blocking collectives  11.2 us (2%)
    all_gather x2, waiting for transfers between devices, side_by_side(): lax.all_gather(both, axis, axis=dim, tiled=True)  193 us
    reduce_scatter x2, waiting for transfers between devices, reduced_to_own(): tiles = lax.psum_scatter(tiles, axes[k], scatter_dimension=0, tiled=True)  78.2 us
    slice x4, local copies, waits for them, and re-layouts, side_by_side(): lax.slice_in_dim(result, at, at + a.shape[along], axis=along)  36.3 us
    dot_general x4, matrix products, fold_block(): jnp.einsum('hqd,' + key_form + '->hqk', queries, key_block, preferred_ele...  24.5 us
    reduce_sum x4, other arithmetic, fold_block(): running_sum = running_sum * shrink + jnp.sum(weights, axis=2)  19.6 us
    dot_general x4, matrix products, fold_block(): jnp.einsum('hqk,' + key_form + '->hqd', weights.astype(jnp.bfloat16), val...  18.3 us
    reshape x2, local copies, waits for them, and re-layouts, reduced_to_own(): tiles = tiles.reshape(*dims, *tiles.shape[1:])  10.2 us
  transfers between devices with their start and end apart: 4, of which 4 were waited for; matrix products, arithmetic and copies ran while one was open for 0% of the time, Pallas kernels for 0%

commit v1 on v0

v1 whole, which is shorter than its diff:
```python
import math

import jax
import jax.numpy as jnp
from jax import lax
from jax.experimental import pallas as pl
from jax.experimental.pallas import tpu as pltpu
from jax.sharding import Mesh
from jax.sharding import PartitionSpec as P

AXES = ("x", "zl", "row", "zh", "y")
MESH = pl.DeviceIdType.MESH
F32, BF16 = jnp.float32, jnp.bfloat16
D = 6144
EPS = 0.25
HD = 128
TOK = 512
HALF = 256
FEAT = 384
GB = 16
SCALE = math.log2(math.e) / math.sqrt(HD)
QB = 256
OWN, OTHER = 0, 1
HERE, RIGHT, LEFT, OPP = 0, 1, 2, 3
N_COPIES = 90


def dot(a, b, dims=((1,), (0,))):
    return lax.dot_general(a, b, (dims, ((), ())), preferred_element_type=F32)


def kernel(
    tok_ref,
    gb_ref,
    w_ref,
    wo_ref,
    out_ref,
    slabs,
    normed,
    w_vm,
    wo_vm,
    acc,
    arrived,
    stats,
    columns,
    outgoing,
    q_vm,
    kv,
    top,
    blended,
    ctx_out,
    ctx,
    partial,
    landed,
    send_sems,
    recv_sems,
    load_sems,
):
    at = {a: lax.axis_index(a) for a in AXES}
    sizes = dict(x=4, zl=4, row=2, zh=2, y=4)

    def shifted(**by):
        return {
            a: lax.rem(at[a] + (by[a] % sizes[a]), sizes[a]) if a in by else at[a] for a in AXES
        }

    mate = shifted(row=1)
    far = shifted(zh=1)
    y_right, y_left, y_opp = shifted(y=1), shifted(y=-1), shifted(y=2)
    x_right, x_left = shifted(x=1), shifted(x=-1)
    z_fwd = [None] + [shifted(zl=d) for d in (1, 2, 3)]
    z_back = [None] + [shifted(zl=-d) for d in (1, 2, 3)]
    copies = []

    def send(src, dst, device):
        i = len(copies)
        copy = pltpu.make_async_remote_copy(
            src_ref=src,
            dst_ref=dst,
            send_sem=send_sems.at[i],
            recv_sem=recv_sems.at[i],
            device_id=device,
            device_id_type=MESH,
        )
        copy.start()
        copies.append(copy)
        return copy

    loads = []

    def load(src, dst):
        copy = pltpu.make_async_copy(src, dst, load_sems.at[len(loads)])
        copy.start()
        loads.append(copy)
        return copy

    own_tok = load(tok_ref, slabs.at[0, pl.ds(0, TOK)])
    own_gb = load(gb_ref, slabs.at[0, pl.ds(TOK, GB)])

    y_of = [at["y"], y_left["y"], y_right["y"], y_opp["y"]]
    head_of = [at["zl"]] + [z_fwd[d]["zl"] for d in (1, 2, 3)]
    w_loads = []
    for slot in range(8):
        zh = at["zh"] if slot < 4 else far["zh"]
        first = (zh * 4 + y_of[slot % 4]) * FEAT
        w_loads.append(
            [
                load(
                    w_ref.at[:, pl.ds(first, FEAT), pl.ds(head_of[d] * HD, HD)],
                    w_vm.at[slot // 2, :, pl.ds((slot % 2) * FEAT, FEAT), pl.ds(d * HD, HD)],
                )
                for d in range(4)
            ]
        )

    barrier = pltpu.get_barrier_semaphore()
    partners = [mate, far, y_right, y_left, y_opp, x_right, x_left, *z_fwd[1:]]
    for p in partners:
        pl.semaphore_signal(barrier, inc=1, device_id=p, device_id_type=MESH)
    pl.semaphore_wait(barrier, len(partners))

    chunks = (pl.ds(0, HALF), pl.ds(HALF, HALF + GB))

    def move(src_slot, dst_slot, chunk, device):
        return send(slabs.at[src_slot, chunks[chunk]], slabs.at[dst_slot, chunks[chunk]], device)

    own_tok.wait()
    own_gb.wait()
    z_in = [move(0, 4, 0, far)]
    l_in, r_in = [None, None], [None, None]
    l_in[0] = move(0, 1, 0, y_right)
    r_in[1] = move(0, 2, 1, y_left)
    z_in.append(move(0, 4, 1, far))
    l_in[1] = move(0, 1, 1, y_right)
    r_in[0] = move(0, 2, 0, y_left)

    rows8 = lax.broadcasted_iota(jnp.int32, (8, FEAT), 0)
    pick_sum = (rows8 < 4).astype(F32).astype(BF16)
    pick_sq = (rows8 >= 4).astype(F32).astype(BF16)
    mine = slabs[0, :TOK, :]
    squares = mine.astype(F32) * mine.astype(F32)
    high = squares.astype(BF16)
    low = (squares - high.astype(F32)).astype(BF16)
    wide = (
        dot(pick_sum, mine, ((1,), (1,)))
        + dot(pick_sq, high, ((1,), (1,)))
        + dot(pick_sq, low, ((1,), (1,)))
    )
    rows = lax.broadcasted_iota(jnp.int32, (8, 128), 0)
    compact = jnp.zeros((8, 128), F32)
    for j in range(4):
        compact = jnp.where(rows % 4 == j, wide[:, j * 128 : (j + 1) * 128], compact)
    stats[0] = compact
    send(stats.at[0], stats.at[1], mate).wait_recv()
    compact = compact + stats[1]
    stats[2] = compact
    send(stats.at[2], stats.at[3], far).wait_recv()

    l_in[0].wait_recv()
    o_in = [move(1, 3, 0, y_right), None]
    r_in[1].wait_recv()
    o_in[1] = move(2, 3, 1, y_left)

    compact = compact + stats[3]
    stats[4] = compact
    st = [
        send(stats.at[4], stats.at[5], y_right),
        send(stats.at[4], stats.at[6], y_left),
        send(stats.at[4], stats.at[7], y_opp),
    ]
    for s in st:
        s.wait_recv()
    compact = compact + stats[5] + stats[6] + stats[7]
    average = compact / D
    mean_below = pltpu.roll(average, 4, axis=0)
    spread = average - mean_below * mean_below
    both = jnp.where(rows < 4, average, lax.rsqrt(spread + EPS))
    columns[...] = jnp.transpose(jnp.concatenate([both] * 16, axis=0))

    def normalize(slot):
        gb = slabs[slot, TOK : TOK + GB, :].astype(F32)
        gain, bias = gb[0:1], gb[8:9]
        for j in range(4):
            x = slabs[slot, j * 128 : (j + 1) * 128, :].astype(F32)
            mean, rstd = columns[:, j : j + 1], columns[:, 4 + j : 5 + j]
            normed[j * 128 : (j + 1) * 128, (slot % 2) * FEAT : (slot % 2 + 1) * FEAT] = (
                (x - mean) * rstd * gain + bias
            ).astype(BF16)

    def project(pair, k):
        product = dot(normed[...], w_vm[pair, k])
        acc[k] = product if pair == 0 else acc[k] + product

    def weights_in(pair):
        for slot in (2 * pair, 2 * pair + 1):
            for c in w_loads[slot]:
                c.wait()

    normalize(0)
    z_in[0].wait_recv()
    zl_in, zr_in = [move(4, 5, 0, y_right), None], [move(4, 6, 0, y_left), None]
    l_in[1].wait_recv()
    normalize(1)
    weights_in(0)
    for k in range(3):
        project(0, k)
    r_in[0].wait_recv()
    normalize(2)
    o_in[0].wait_recv()
    o_in[1].wait_recv()
    normalize(3)
    weights_in(1)
    for k in range(3):
        project(1, k)

    wo_loads = []
    y_dest = [at["y"], y_right["y"], y_left["y"], y_opp["y"]]
    for b in range(8):
        zh = at["zh"] if b < 4 else far["zh"]
        first = (zh * 4 + y_dest[b % 4]) * FEAT
        for d in range(4):
            wo_loads.append(
                load(
                    wo_ref.at[pl.ds(head_of[d] * HD, HD), pl.ds(first, FEAT)],
                    wo_vm.at[b, pl.ds(d * HD, HD)],
                )
            )

    zl_in[0].wait_recv()
    zo_in = [move(5, 7, 0, y_right), None]
    z_in[1].wait_recv()
    zr_in[1] = move(4, 6, 1, y_left)
    zl_in[1] = move(4, 5, 1, y_right)
    normalize(4)
    zr_in[1].wait_recv()
    zo_in[1] = move(6, 7, 1, y_left)
    zl_in[1].wait_recv()
    normalize(5)
    weights_in(2)
    for k in range(3):
        project(2, k)
    zr_in[0].wait_recv()
    normalize(6)
    zo_in[0].wait_recv()
    zo_in[1].wait_recv()
    normalize(7)
    weights_in(3)

    keep = pl.ds(at["row"] * HALF, HALF)
    give = pl.ds(mate["row"] * HALF, HALF)
    halves = {}
    for k in (1, 2, 0):
        project(3, k)
        halves[k] = send(acc.at[k, give], arrived.at[k], mate)
    z_sent = {}
    for k in (1, 2, 0):
        halves[k].wait_recv()
        whole = acc[k, keep, :] + arrived[k]
        if k == 0:
            whole = whole * SCALE
        whole = whole.astype(BF16)
        for d in (1, 2, 3):
            outgoing[k, d - 1] = whole[:, d * HD : (d + 1) * HD]
            target = q_vm.at[d] if k == 0 else kv.at[0, 0, k - 1, d]
            z_sent[k, d] = send(outgoing.at[k, d - 1], target, z_fwd[d])
        if k == 0:
            q_vm[0] = whole[:, :HD]
        else:
            kv[0, 0, k - 1, 0] = whole[:, :HD]

    right_in, left_in, opp_in, mate_in = {}, {}, {}, {}

    def to_mate(side, d):
        mate_in[side, d] = send(kv.at[side, 0, :, d], kv.at[side, 1, :, d], mate)

    def spread_own(d):
        left_in[d] = send(kv.at[0, 0, :, d], kv.at[1, 0, :, d], x_right)
        right_in[d] = send(kv.at[0, 0, :, d], kv.at[2, 0, :, d], x_left)
        to_mate(0, d)

    def pass_on(d):
        left_in[d].wait_recv()
        if d < 2:
            opp_in[d] = send(kv.at[1, 0, :, d], kv.at[3, 0, :, d], x_right)
        to_mate(1, d)
        right_in[d].wait_recv()
        if d >= 2:
            opp_in[d] = send(kv.at[2, 0, :, d], kv.at[3, 0, :, d], x_left)
        to_mate(2, d)

    spread_own(0)
    for d in (1, 2, 3):
        z_sent[1, d].wait_recv()
        z_sent[2, d].wait_recv()
        spread_own(d)
        if d >= 2:
            pass_on(d - 2)
    for d in (1, 2, 3):
        z_sent[0, d].wait_recv()

    per_slot = 4 * HALF
    n_q = per_slot // QB
    ones = jnp.ones((per_slot, HD), BF16)

    def attend(side, core, first):
        def block(i, carry):
            at_q = pl.ds(pl.multiple_of(i * QB, QB), QB)
            q = q_vm[...].reshape(per_slot, HD) if n_q == 1 else q_vm[i]
            keys = kv[side, core, 0].reshape(per_slot, HD)
            values = kv[side, core, 1].reshape(per_slot, HD)
            scores = dot(q, keys, ((1,), (1,)))
            best = jnp.max(scores, axis=1, keepdims=True)
            if not first:
                before = top[at_q, 0:1]
                best = jnp.maximum(before, best)
            weights = jnp.exp2(scores - best).astype(BF16)
            product = dot(weights, jnp.concatenate([values, ones], axis=1))
            if first:
                blended[at_q, :] = product
            else:
                blended[at_q, :] = blended[at_q, :] * jnp.exp2(before - best) + product
            top[at_q, :] = jnp.broadcast_to(best, (QB, 128))
            return carry

        lax.fori_loop(0, n_q, block, 0)

    attend(0, 0, True)
    for d in range(4):
        mate_in[0, d].wait_recv()
    pass_on(2)
    attend(0, 1, False)
    pass_on(3)
    attend(1, 0, False)
    attend(2, 0, False)
    for side in (1, 2):
        for d in range(4):
            mate_in[side, d].wait_recv()
    for d in range(4):
        opp_in[d].wait_recv()
        to_mate(3, d)
    attend(1, 1, False)
    attend(2, 1, False)
    attend(3, 0, False)
    for d in range(4):
        mate_in[3, d].wait_recv()
    attend(3, 1, False)

    c_in = {}
    for d in (1, 2, 3, 0):
        rows_d = slice(d * HALF, (d + 1) * HALF)
        value = (blended[rows_d, :HD] / blended[rows_d, HD:]).astype(BF16)
        if d == 0:
            ctx[0, 0] = value
        else:
            ctx_out[d - 1] = value
            c_in[d] = send(ctx_out.at[d - 1], ctx.at[0, d], z_back[d])
    m_in = [send(ctx.at[0, 0], ctx.at[1, 0], mate)]
    for d in (1, 2, 3):
        c_in[d].wait_recv()
        m_in.append(send(ctx.at[0, d], ctx.at[1, d], mate))
    for c in wo_loads:
        c.wait()

    def product(z, y, j):
        a = jnp.concatenate([ctx[j, d] for d in range(4)], axis=1)
        return dot(a, wo_vm[4 * z + y])

    out_in = {}
    names = {}

    def push(name, j, value, device):
        n = names.setdefault(name, len(names))
        partial[n, j] = value.astype(BF16)
        out_in[name, j] = send(partial.at[n, j], landed.at[n, j], device)

    def got(name, j):
        out_in[name, j].wait_recv()
        return landed[names[name], j].astype(F32)

    for j in (0, 1):
        if j == 1:
            for m in m_in:
                m.wait_recv()
        push("o_opp", j, product(OTHER, OPP, j), y_right)
        push("o_right", j, product(OTHER, LEFT, j), y_left)
    for j in (0, 1):
        push("w_opp", j, product(OWN, OPP, j), y_left)
    for j in (0, 1):
        push("o_left", j, product(OTHER, RIGHT, j) + got("o_opp", j), y_right)
    for j in (0, 1):
        push("w_left", j, product(OWN, RIGHT, j), y_right)
    for j in (0, 1):
        push("w_right", j, product(OWN, LEFT, j) + got("w_opp", j), y_left)
        push("z", j, product(OTHER, HERE, j) + got("o_left", j) + got("o_right", j), far)
    for j in (0, 1):
        rows_j = keep if j == 0 else give
        total = product(OWN, HERE, j) + got("w_left", j) + got("w_right", j)
        total = total + got("z", j) + slabs[0, rows_j, :].astype(F32)
        out_ref[rows_j, :] = total.astype(BF16)
    for copy in copies:
        copy.wait_send()


def body(tokens, ln_gain, ln_bias, w_qkv, w_out):
    gb = jnp.concatenate(
        [jnp.broadcast_to(ln_gain[None], (8, FEAT)), jnp.broadcast_to(ln_bias[None], (8, FEAT))]
    )
    any_spec = pl.BlockSpec(memory_space=pl.ANY)
    return pl.pallas_call(
        kernel,
        out_shape=jax.ShapeDtypeStruct((TOK, FEAT), BF16),
        in_specs=[any_spec] * 4,
        out_specs=pl.BlockSpec(memory_space=pltpu.VMEM),
        scratch_shapes=[
            pltpu.VMEM((8, TOK + GB, FEAT), BF16),
            pltpu.VMEM((TOK, 2 * FEAT), BF16),
            pltpu.VMEM((4, 3, 2 * FEAT, 4 * HD), BF16),
            pltpu.VMEM((8, 4 * HD, FEAT), BF16),
            pltpu.VMEM((3, TOK, 4 * HD), F32),
            pltpu.VMEM((3, HALF, 4 * HD), F32),
            pltpu.VMEM((8, 8, 128), F32),
            pltpu.VMEM((128, 128), F32),
            pltpu.VMEM((3, 3, HALF, HD), BF16),
            pltpu.VMEM((4, HALF, HD), BF16),
            pltpu.VMEM((4, 2, 2, 4, HALF, HD), BF16),
            pltpu.VMEM((4 * HALF, 128), F32),
            pltpu.VMEM((4 * HALF, 2 * HD), F32),
            pltpu.VMEM((3, HALF, HD), BF16),
            pltpu.VMEM((2, 4, HALF, HD), BF16),
            pltpu.VMEM((7, 2, HALF, FEAT), BF16),
            pltpu.VMEM((7, 2, HALF, FEAT), BF16),
            pltpu.SemaphoreType.DMA((N_COPIES,)),
            pltpu.SemaphoreType.DMA((N_COPIES,)),
            pltpu.SemaphoreType.DMA((66,)),
        ],
        compiler_params=pltpu.CompilerParams(
            collective_id=0, has_side_effects=True, vmem_limit_bytes=60 * 2**20
        ),
    )(tokens, gb, w_qkv, w_out)


def solution(mesh):
    finer = Mesh(mesh.devices.reshape(4, 4, 2, 2, 4), AXES)
    seq, row_col, col = ("x", "zl"), ("row", "zh", "y"), ("zh", "y")
    in_specs = (P(seq, row_col), P(row_col), P(row_col), P(None, "row", col), P(col, "row"))
    return jax.shard_map(
        body, mesh=finer, in_specs=in_specs, out_specs=P(seq, row_col), check_vma=False
    )
```

time: 456 us -> 156 us (0.34)
  waiting for transfers between devices: 271 us -> 0 us
  Pallas kernels: 0 us -> 150 us
  local copies, waits for them, and re-layouts: 63.8 us -> 3.14 us
  matrix products: 52 us -> 0 us
  other arithmetic: 39.9 us -> 0.6 us
  between operations: 13.2 us -> 0.01 us
  blocking collectives: 11.2 us -> 0 us
    all_gather x2 -> x0, waiting for transfers between devices: 193 us -> none  [side_by_side(): lax.all_gather(both, axis, axis=dim, tiled=True)]
    pallas_call x0 -> x1, Pallas kernels: none -> 150 us  [body(): pl.pallas_call(kernel, out_shape=jax.ShapeDtypeStruct((TOK, FEAT), BF16),...]
    reduce_scatter x2 -> x0, waiting for transfers between devices: 78.2 us -> none  [reduced_to_own(): tiles = lax.psum_scatter(tiles, axes[k], scatter_dimension=0, tiled=True)]
    dot_general x10 -> x0, matrix products: 52 us -> none  [the longest x4 24.5 us: fold_block(): jnp.einsum('hqd,' + key_form + '->hqk', queries, key_block, preferred_ele...]
    slice x6 -> x0, local copies, waits for them, and re-layouts: 38.3 us -> none  [the longest x4 36.3 us: side_by_side(): lax.slice_in_dim(result, at, at + a.shape[along], axis=along)]
    reduce_sum x6 -> x0, other arithmetic: 28 us -> none  [the longest x4 19.6 us: fold_block(): running_sum = running_sum * shrink + jnp.sum(weights, axis=2)]
    all_to_all x2 -> x0, blocking collectives: 11.2 us -> none  [the longest x1 7.11 us: sent_and_summed(): lax.all_to_all(tiles, axis, split_axis=0, concat_axis=0, tiled=True)]
    reshape x3 -> x0, local copies, waits for them, and re-layouts: 10.8 us -> none  [the longest x2 10.2 us: reduced_to_own(): tiles = tiles.reshape(*dims, *tiles.shape[1:])]
  transfers between devices with their start and end apart: 4 -> 0, of which waited for: 4 -> 0; matrix products, arithmetic and copies ran while one was open for 0% -> 0% of each run, Pallas kernels for 0% -> 0%
where the time goes in v1:
time: 156 us; the launch traced here: 154 us
  Pallas kernels  150 us (96%)
  local copies, waits for them, and re-layouts  3.14 us (2%)
    pallas_call x1, Pallas kernels, body(): pl.pallas_call(kernel, out_shape=jax.ShapeDtypeStruct((TOK, FEAT), BF16),...  150 us

profile of v1, /device:TPU:1, one launch (start us, length us, event | category | flops | bytes accessed | tf_op | source)
XLA Modules:
  0.0 154.0 jit_solution(17856035477792316163)
XLA Ops:
  0.0 0.7 broadcast_in_dim.4
  0.7 0.7 broadcast_in_dim.5
  1.4 0.6 pad_maximum_fusion.gb_ref
  2.0 150.2 %shard_map.55 = bf16[512,384]{1,0:T(8,128)(2,1)} custom-call(bf16[512,384]{1,0:T(8,128)(2,1)} %tok_ref.1, bf16[16,384]{1,0:T(8,128)(2,1)} %pad_maximum_fusion.gb_ref, bf16[3,3072,512]{2,1,0:T(8,128)(2,1)} %w_ref.1, bf16[512,3072]{1,0:T(8,128)(2,1)} %wo_ref.1), custom_call_target="tpu_custom_call" | custom-call | tf_op jit(solution)/shard_map/pallas_call | solution.py:409
  152.2 1.8 %copy.7 = bf16[512,384]{1,0:T(8,128)(2,1)} copy(bf16[512,384]{1,0:T(8,128)(2,1)} %shard_map.55) | data formatting | bytes 786432

commit v2 on v1

v2 whole, which is shorter than its diff:
```python
import math

import jax
import jax.numpy as jnp
from jax import lax
from jax.experimental import pallas as pl
from jax.experimental.pallas import tpu as pltpu
from jax.sharding import Mesh
from jax.sharding import PartitionSpec as P

AXES = ("x", "zl", "row", "zh", "y")
MESH = pl.DeviceIdType.MESH
F32, BF16 = jnp.float32, jnp.bfloat16
D = 6144
EPS = 0.25
HD = 128
TOK = 512
QUARTER = 128
HALF = 256
FEAT = 384
GB = 16
SCALE = math.log2(math.e) / math.sqrt(HD)
KEYS = 512
OWN, OTHER = 0, 1
HERE, RIGHT, LEFT, OPP = 0, 1, 2, 3
N_COPIES = 140


def dot(a, b, dims=((1,), (0,))):
    return lax.dot_general(a, b, (dims, ((), ())), preferred_element_type=F32)


def kernel(
    tok_ref,
    gb_ref,
    w_ref,
    wo_ref,
    out_ref,
    slabs,
    normed,
    w_vm,
    wo_vm,
    acc,
    arrived,
    stats,
    columns,
    outgoing,
    q_vm,
    kv,
    top,
    blended,
    ctx_out,
    ctx,
    partial,
    landed,
    send_sems,
    recv_sems,
    load_sems,
):
    at = {a: lax.axis_index(a) for a in AXES}
    sizes = dict(x=4, zl=4, row=2, zh=2, y=4)

    def shifted(**by):
        return {
            a: lax.rem(at[a] + (by[a] % sizes[a]), sizes[a]) if a in by else at[a] for a in AXES
        }

    mate = shifted(row=1)
    far = shifted(zh=1)
    far_mate = shifted(zh=1, row=1)
    y_right, y_left, y_opp = shifted(y=1), shifted(y=-1), shifted(y=2)
    x_right, x_left = shifted(x=1), shifted(x=-1)
    z_fwd = [None] + [shifted(zl=d) for d in (1, 2, 3)]
    z_back = [None] + [shifted(zl=-d) for d in (1, 2, 3)]
    copies = []

    def send(src, dst, device):
        i = len(copies)
        copy = pltpu.make_async_remote_copy(
            src_ref=src,
            dst_ref=dst,
            send_sem=send_sems.at[i],
            recv_sem=recv_sems.at[i],
            device_id=device,
            device_id_type=MESH,
        )
        copy.start()
        copies.append(copy)
        return copy

    loads = []

    def load(src, dst):
        copy = pltpu.make_async_copy(src, dst, load_sems.at[len(loads)])
        copy.start()
        loads.append(copy)
        return copy

    own_tok = load(tok_ref, slabs.at[0, pl.ds(GB, TOK)])
    own_gb = load(gb_ref, slabs.at[0, pl.ds(0, GB)])

    y_of = [at["y"], y_left["y"], y_right["y"], y_opp["y"]]
    head_of = [at["zl"]] + [z_fwd[d]["zl"] for d in (1, 2, 3)]
    w_loads = []
    for slot in range(8):
        zh = at["zh"] if slot < 4 else far["zh"]
        first = (zh * 4 + y_of[slot % 4]) * FEAT
        w_loads.append(
            [
                load(
                    w_ref.at[:, pl.ds(first, FEAT), pl.ds(head_of[d] * HD, HD)],
                    w_vm.at[slot // 2, :, pl.ds((slot % 2) * FEAT, FEAT), pl.ds(d * HD, HD)],
                )
                for d in range(4)
            ]
        )

    barrier = pltpu.get_barrier_semaphore()
    partners = [mate, far, far_mate, y_right, y_left, y_opp, x_right, x_left, *z_fwd[1:]]
    for p in partners:
        pl.semaphore_signal(barrier, inc=1, device_id=p, device_id_type=MESH)
    own_tok.wait()
    own_gb.wait()

    rows8 = lax.broadcasted_iota(jnp.int32, (8, FEAT), 0)
    pick_sum = (rows8 < 4).astype(F32).astype(BF16)
    pick_sq = (rows8 >= 4).astype(F32).astype(BF16)
    mine = slabs[0, GB:, :]
    squares = mine.astype(F32) * mine.astype(F32)
    high = squares.astype(BF16)
    low = (squares - high.astype(F32)).astype(BF16)
    wide = (
        dot(pick_sum, mine, ((1,), (1,)))
        + dot(pick_sq, high, ((1,), (1,)))
        + dot(pick_sq, low, ((1,), (1,)))
    )
    rows = lax.broadcasted_iota(jnp.int32, (8, 128), 0)
    compact = jnp.zeros((8, 128), F32)
    for j in range(4):
        compact = jnp.where(rows % 4 == j, wide[:, j * 128 : (j + 1) * 128], compact)
    stats[0] = compact
    pl.semaphore_wait(barrier, len(partners))
    st = [
        send(stats.at[0], stats.at[1], mate),
        send(stats.at[0], stats.at[2], far),
        send(stats.at[0], stats.at[3], far_mate),
    ]

    chunks = [pl.ds(0, GB + QUARTER)] + [pl.ds(GB + i * QUARTER, QUARTER) for i in (1, 2, 3)]

    def move(src_slot, dst_slot, chunk, device):
        return send(slabs.at[src_slot, chunks[chunk]], slabs.at[dst_slot, chunks[chunk]], device)

    from_left, from_right, from_opp = [{}, {}], [{}, {}], [{}, {}]

    def offer(z, i):
        from_left[z][i] = move(4 * z, 4 * z + 1, i, y_right)
        from_right[z][i] = move(4 * z, 4 * z + 2, i, y_left)

    def relay(z, i):
        if i % 2 == 0:
            from_left[z][i].wait_recv()
            from_opp[z][i] = move(4 * z + 1, 4 * z + 3, i, y_right)
        else:
            from_right[z][i].wait_recv()
            from_opp[z][i] = move(4 * z + 2, 4 * z + 3, i, y_left)

    z_in = []
    for i in range(4):
        z_in.append(move(0, 4, i, far))
        offer(OWN, i)

    def offer_far(i):
        z_in[i].wait_recv()
        offer(OTHER, i)

    for s in st:
        s.wait_recv()
    compact = compact + stats[1] + stats[2] + stats[3]
    stats[4] = compact
    st = [
        send(stats.at[4], stats.at[5], y_right),
        send(stats.at[4], stats.at[6], y_left),
        send(stats.at[4], stats.at[7], y_opp),
    ]
    relay(OWN, 0)
    relay(OWN, 1)
    offer_far(0)
    relay(OWN, 2)
    relay(OWN, 3)
    for s in st:
        s.wait_recv()
    compact = compact + stats[5] + stats[6] + stats[7]
    average = compact / D
    mean_below = pltpu.roll(average, 4, axis=0)
    spread = average - mean_below * mean_below
    both = jnp.where(rows < 4, average, lax.rsqrt(spread + EPS))
    columns[...] = jnp.transpose(jnp.concatenate([both] * 16, axis=0))

    def normalize(slot, groups=range(4)):
        gb = slabs[slot, :GB, :].astype(F32)
        gain, bias = gb[0:1], gb[8:9]
        for j in groups:
            x = slabs[slot, GB + j * 128 : GB + (j + 1) * 128, :].astype(F32)
            mean, rstd = columns[:, j : j + 1], columns[:, 4 + j : 5 + j]
            normed[j * 128 : (j + 1) * 128, (slot % 2) * FEAT : (slot % 2 + 1) * FEAT] = (
                (x - mean) * rstd * gain + bias
            ).astype(BF16)

    def project(pair, k, rows=slice(0, TOK)):
        product = dot(normed[rows], w_vm[pair, k])
        acc[k, rows] = product if pair == 0 else acc[k, rows] + product

    def weights_in(pair):
        for slot in (2 * pair, 2 * pair + 1):
            for c in w_loads[slot]:
                c.wait()

    normalize(0)
    offer_far(1)
    for i in (1, 3):
        from_left[OWN][i].wait_recv()
    normalize(1)
    weights_in(0)
    for k in range(3):
        project(0, k)
    offer_far(2)
    relay(OTHER, 0)
    for i in (0, 2):
        from_right[OWN][i].wait_recv()
    normalize(2)
    for i in range(4):
        from_opp[OWN][i].wait_recv()
    normalize(3)
    relay(OTHER, 1)
    weights_in(1)
    for k in range(3):
        project(1, k)

    wo_loads = []
    y_dest = [at["y"], y_right["y"], y_left["y"], y_opp["y"]]
    for b in range(8):
        zh = at["zh"] if b < 4 else far["zh"]
        first = (zh * 4 + y_dest[b % 4]) * FEAT
        for d in range(4):
            wo_loads.append(
                load(
                    wo_ref.at[pl.ds(head_of[d] * HD, HD), pl.ds(first, FEAT)],
                    wo_vm.at[b, pl.ds(d * HD, HD)],
                )
            )

    offer_far(3)
    relay(OTHER, 2)
    normalize(4)
    relay(OTHER, 3)
    for i in (1, 3):
        from_left[OTHER][i].wait_recv()
    normalize(5)
    weights_in(2)
    for k in range(3):
        project(2, k)
    for i in (0, 2):
        from_right[OTHER][i].wait_recv()
    normalize(6)
    weights_in(3)

    def kv_part(side, core, d, p):
        return kv.at[side, core, :, d, pl.ds(p * QUARTER, QUARTER)]

    z_kv, z_q = {}, {}
    right_in, left_in, opp_in, mate_in = {}, {}, {}, {}

    def to_mate(side, d, p):
        mate_in[side, d, p] = send(kv_part(side, 0, d, p), kv_part(side, 1, d, p), mate)

    def spread_own(d, p):
        left_in[d, p] = send(kv_part(0, 0, d, p), kv_part(1, 0, d, p), x_right)
        right_in[d, p] = send(kv_part(0, 0, d, p), kv_part(2, 0, d, p), x_left)
        to_mate(0, d, p)

    def pass_on(d, p):
        left_in[d, p].wait_recv()
        if (d + p) % 2 == 0:
            opp_in[d, p] = send(kv_part(1, 0, d, p), kv_part(3, 0, d, p), x_right)
        to_mate(1, d, p)
        right_in[d, p].wait_recv()
        if (d + p) % 2 == 1:
            opp_in[d, p] = send(kv_part(2, 0, d, p), kv_part(3, 0, d, p), x_left)
        to_mate(2, d, p)

    def z_arrived(d, p):
        z_kv[d, p].wait_recv()
        spread_own(d, p)

    for p in (0, 1):
        for i in (2 * p, 2 * p + 1):
            from_opp[OTHER][i].wait_recv()
        normalize(7, (2 * p, 2 * p + 1))
        keep_p = pl.ds(p * HALF + at["row"] * QUARTER, QUARTER)
        give_p = pl.ds(p * HALF + mate["row"] * QUARTER, QUARTER)
        rows_p = pl.ds(p * QUARTER, QUARTER)
        halves = {}
        for k in (1, 2, 0):
            project(3, k, slice(p * HALF, (p + 1) * HALF))
            halves[k] = send(acc.at[k, give_p], arrived.at[p, k], mate)
        for k in (1, 2, 0):
            halves[k].wait_recv()
            whole = acc[k, keep_p, :] + arrived[p, k]
            if k == 0:
                whole = whole * SCALE
            whole = whole.astype(BF16)
            for d in (1, 2, 3):
                outgoing[p, d - 1, k] = whole[:, d * HD : (d + 1) * HD]
            if k == 0:
                q_vm[0, rows_p] = whole[:, :HD]
                for d in (1, 2, 3):
                    z_q[d, p] = send(outgoing.at[p, d - 1, 0], q_vm.at[d, rows_p], z_fwd[d])
            else:
                kv[0, 0, k - 1, 0, rows_p] = whole[:, :HD]
            if k == 2:
                for d in (1, 2, 3):
                    z_kv[d, p] = send(
                        outgoing.at[p, d - 1, pl.ds(1, 2)], kv_part(0, 0, d, p), z_fwd[d]
                    )
                spread_own(0, p)

    z_arrived(1, 0)
    z_arrived(2, 0)
    pass_on(0, 0)
    z_arrived(3, 0)
    pass_on(0, 1)
    z_arrived(1, 1)
    pass_on(1, 0)
    z_arrived(2, 1)
    pass_on(2, 0)
    z_arrived(3, 1)
    pass_on(3, 0)
    for p in (0, 1):
        for d in (1, 2, 3):
            z_q[d, p].wait_recv()

    ones = jnp.ones((KEYS, HD), BF16)
    n_q = 4 * HALF

    def attend(slots, begin, size, first):
        at_q = pl.ds(begin, size)
        q = q_vm[begin // HALF : (begin + size) // HALF].reshape(size, HD)
        best = None if first else top[at_q, :]
        total = None if first else blended[at_q, :]
        steps = [(slot, i) for slot in slots for i in range(n_q // KEYS)]
        d_step = KEYS // HALF

        def piece(step, k):
            (side, core), i = step
            return kv[side, core, k, i * d_step : (i + 1) * d_step].reshape(KEYS, HD)

        def lanes(values):
            return [values[:, c : c + HD] for c in range(0, values.shape[1], HD)]

        scores = dot(q, piece(steps[0], 0), ((1,), (1,)))
        for n, step in enumerate(steps):
            following = None
            if n + 1 < len(steps):
                following = dot(q, piece(steps[n + 1], 0), ((1,), (1,)))
            parts = lanes(scores)
            high = parts[0]
            for part in parts[1:]:
                high = jnp.maximum(high, part)
            now = jnp.broadcast_to(jnp.max(high, axis=1, keepdims=True), (size, HD))
            if best is not None:
                now = jnp.maximum(best, now)
            weights = [jnp.exp2(part - now).astype(BF16) for part in parts]
            product = dot(
                jnp.concatenate(weights, axis=1),
                jnp.concatenate([piece(step, 1), ones], axis=1),
            )
            if best is None:
                total = product
            else:
                shrink = jnp.exp2(best - now)
                total = jnp.concatenate([part * shrink for part in lanes(total)], axis=1) + product
            best, scores = now, following
        blended[at_q, :] = total
        top[at_q, :] = best

    def mates_in(side):
        for d in range(4):
            for p in (0, 1):
                mate_in[side, d, p].wait_recv()

    attend([(0, 0)], 0, n_q, True)
    pass_on(1, 1)
    pass_on(2, 1)
    mates_in(0)
    attend([(0, 1)], 0, n_q, False)
    pass_on(3, 1)
    attend([(1, 0), (2, 0)], 0, n_q, False)
    for d in range(4):
        for p in (0, 1):
            opp_in[d, p].wait_recv()
            to_mate(3, d, p)
    for side in (1, 2, 3):
        mates_in(side)

    c_in = {}
    for begin in (2 * HALF, 0):
        attend([(1, 1), (2, 1), (3, 0), (3, 1)], begin, 2 * HALF, False)
        for d in (begin // HALF + 1, begin // HALF):
            rows_d = slice(d * HALF, (d + 1) * HALF)
            value = (blended[rows_d, :HD] / blended[rows_d, HD:]).astype(BF16)
            if d == 0:
                ctx[0, 0] = value
            else:
                ctx_out[d - 1] = value
                c_in[d] = send(ctx_out.at[d - 1], ctx.at[0, d], z_back[d])
    m_in = [send(ctx.at[0, 0], ctx.at[1, 0], mate)]
    for d in (3, 2, 1):
        c_in[d].wait_recv()
        m_in.append(send(ctx.at[0, d], ctx.at[1, d], mate))
    for c in wo_loads:
        c.wait()

    def product(z, y, j):
        a = jnp.concatenate([ctx[j, d] for d in range(4)], axis=1)
        return dot(a, wo_vm[4 * z + y])

    out_in = {}
    names = {}

    def push(name, j, value, device):
        n = names.setdefault(name, len(names))
        partial[n, j] = value.astype(BF16)
        out_in[name, j] = send(partial.at[n, j], landed.at[n, j], device)

    def got(name, j):
        out_in[name, j].wait_recv()
        return landed[names[name], j].astype(F32)

    for j in (0, 1):
        if j == 1:
            for m in m_in:
                m.wait_recv()
        push("o_opp", j, product(OTHER, OPP, j), y_right)
        push("o_right", j, product(OTHER, LEFT, j), y_left)
    for j in (0, 1):
        push("w_opp", j, product(OWN, OPP, j), y_left)
    for j in (0, 1):
        push("o_left", j, product(OTHER, RIGHT, j) + got("o_opp", j), y_right)
    for j in (0, 1):
        push("w_left", j, product(OWN, RIGHT, j), y_right)
    for j in (0, 1):
        push("w_right", j, product(OWN, LEFT, j) + got("w_opp", j), y_left)
        push("z", j, product(OTHER, HERE, j) + got("o_left", j) + got("o_right", j), far)
    for j in (0, 1):
        total = product(OWN, HERE, j) + got("w_left", j) + got("w_right", j) + got("z", j)
        core = at["row"] if j == 0 else mate["row"]
        for p in (0, 1):
            first = p * HALF + core * QUARTER
            piece = total[p * QUARTER : (p + 1) * QUARTER]
            own = slabs[0, pl.ds(GB + first, QUARTER), :].astype(F32)
            out_ref[pl.ds(first, QUARTER), :] = (piece + own).astype(BF16)
    for copy in copies:
        copy.wait_send()


def body(tokens, ln_gain, ln_bias, w_qkv, w_out):
    gb = jnp.concatenate(
        [jnp.broadcast_to(ln_gain[None], (8, FEAT)), jnp.broadcast_to(ln_bias[None], (8, FEAT))]
    )
    any_spec = pl.BlockSpec(memory_space=pl.ANY)
    return pl.pallas_call(
        kernel,
        out_shape=jax.ShapeDtypeStruct((TOK, FEAT), BF16),
        in_specs=[any_spec] * 4,
        out_specs=pl.BlockSpec(memory_space=pltpu.VMEM),
        scratch_shapes=[
            pltpu.VMEM((8, TOK + GB, FEAT), BF16),
            pltpu.VMEM((TOK, 2 * FEAT), BF16),
            pltpu.VMEM((4, 3, 2 * FEAT, 4 * HD), BF16),
            pltpu.VMEM((8, 4 * HD, FEAT), BF16),
            pltpu.VMEM((3, TOK, 4 * HD), F32),
            pltpu.VMEM((2, 3, QUARTER, 4 * HD), F32),
            pltpu.VMEM((8, 8, 128), F32),
            pltpu.VMEM((128, 128), F32),
            pltpu.VMEM((2, 3, 3, QUARTER, HD), BF16),
            pltpu.VMEM((4, HALF, HD), BF16),
            pltpu.VMEM((4, 2, 2, 4, HALF, HD), BF16),
            pltpu.VMEM((4 * HALF, 128), F32),
            pltpu.VMEM((4 * HALF, 2 * HD), F32),
            pltpu.VMEM((3, HALF, HD), BF16),
            pltpu.VMEM((2, 4, HALF, HD), BF16),
            pltpu.VMEM((7, 2, HALF, FEAT), BF16),
            pltpu.VMEM((7, 2, HALF, FEAT), BF16),
            pltpu.SemaphoreType.DMA((N_COPIES,)),
            pltpu.SemaphoreType.DMA((N_COPIES,)),
            pltpu.SemaphoreType.DMA((66,)),
        ],
        compiler_params=pltpu.CompilerParams(
            collective_id=0, has_side_effects=True, vmem_limit_bytes=60 * 2**20
        ),
    )(tokens, gb, w_qkv, w_out)


def solution(mesh):
    finer = Mesh(mesh.devices.reshape(4, 4, 2, 2, 4), AXES)
    seq, row_col, col = ("x", "zl"), ("row", "zh", "y"), ("zh", "y")
    in_specs = (P(seq, row_col), P(row_col), P(row_col), P(None, "row", col), P(col, "row"))
    return jax.shard_map(
        body, mesh=finer, in_specs=in_specs, out_specs=P(seq, row_col), check_vma=False
    )
```

time: 156 us -> 124 us (0.79); the launches traced: 154 us -> 124 us
  Pallas kernels: 150 us -> 120 us
    pallas_call x1, Pallas kernels: 150 us -> 120 us  [body(): pl.pallas_call(kernel, out_shape=jax.ShapeDtypeStruct((TOK, FEAT), BF16),...]
where the time goes in v2:
time: 124 us
  Pallas kernels  120 us (97%)
  local copies, waits for them, and re-layouts  3.14 us (3%)
    pallas_call x1, Pallas kernels, body(): pl.pallas_call(kernel, out_shape=jax.ShapeDtypeStruct((TOK, FEAT), BF16),...  120 us

profile of v2, /device:TPU:1, one launch (start us, length us, event | category | flops | bytes accessed | tf_op | source)
XLA Modules:
  0.0 123.7 jit_solution(58973947625756402)
XLA Ops:
  0.0 0.7 broadcast_in_dim.4
  0.7 0.7 broadcast_in_dim.5
  1.4 0.6 pad_maximum_fusion.gb_ref
  2.0 119.9 %shard_map.55 = bf16[512,384]{1,0:T(8,128)(2,1)} custom-call(bf16[512,384]{1,0:T(8,128)(2,1)} %tok_ref.1, bf16[16,384]{1,0:T(8,128)(2,1)} %pad_maximum_fusion.gb_ref, bf16[3,3072,512]{2,1,0:T(8,128)(2,1)} %w_ref.1, bf16[512,3072]{1,0:T(8,128)(2,1)} %wo_ref.1), custom_call_target="tpu_custom_call" | custom-call | tf_op jit(solution)/shard_map/pallas_call | solution.py:472
  121.9 1.8 %copy.7 = bf16[512,384]{1,0:T(8,128)(2,1)} copy(bf16[512,384]{1,0:T(8,128)(2,1)} %shard_map.55) | data formatting | bytes 786432

commit v3 on v2

--- a/solution.py
+++ b/solution.py
@@ -32,7 +32,8 @@
 
 def kernel(
     tok_ref,
-    gb_ref,
+    gain_ref,
+    bias_ref,
     w_ref,
     wo_ref,
     out_ref,
@@ -40,6 +41,7 @@
     normed,
     w_vm,
     wo_vm,
+    wo_far,
     acc,
     arrived,
     stats,
@@ -56,6 +58,8 @@
     send_sems,
     recv_sems,
     load_sems,
+    chain_send,
+    chain_recv,
 ):
     at = {a: lax.axis_index(a) for a in AXES}
     sizes = dict(x=4, zl=4, row=2, zh=2, y=4)
@@ -72,6 +76,9 @@
     x_right, x_left = shifted(x=1), shifted(x=-1)
     z_fwd = [None] + [shifted(zl=d) for d in (1, 2, 3)]
     z_back = [None] + [shifted(zl=-d) for d in (1, 2, 3)]
+    far_back = [shifted(zh=1, zl=-d) for d in range(4)]
+    z_prev = dict(at, zl=z_back[1]["zl"], zh=jnp.where(at["zl"] == 0, far["zh"], at["zh"]))
+    z_next = dict(at, zl=z_fwd[1]["zl"], zh=jnp.where(at["zl"] == 3, far["zh"], at["zh"]))
     copies = []
 
     def send(src, dst, device):
@@ -97,7 +104,11 @@
         return copy
 
     own_tok = load(tok_ref, slabs.at[0, pl.ds(GB, TOK)])
-    own_gb = load(gb_ref, slabs.at[0, pl.ds(0, GB)])
+    slabs[0, :GB, :] = jnp.where(
+        lax.broadcasted_iota(jnp.int32, (GB, FEAT), 0) < 8,
+        jnp.broadcast_to(gain_ref[...].astype(F32), (GB, FEAT)),
+        jnp.broadcast_to(bias_ref[...].astype(F32), (GB, FEAT)),
+    ).astype(BF16)
 
     y_of = [at["y"], y_left["y"], y_right["y"], y_opp["y"]]
     head_of = [at["zl"]] + [z_fwd[d]["zl"] for d in (1, 2, 3)]
@@ -116,11 +127,10 @@
         )
 
     barrier = pltpu.get_barrier_semaphore()
-    partners = [mate, far, far_mate, y_right, y_left, y_opp, x_right, x_left, *z_fwd[1:]]
+    partners = [mate, far, far_mate, y_right, y_left, y_opp, x_right, x_left, *z_fwd[1:], *far_back[1:]]
     for p in partners:
         pl.semaphore_signal(barrier, inc=1, device_id=p, device_id_type=MESH)
     own_tok.wait()
-    own_gb.wait()
 
     rows8 = lax.broadcasted_iota(jnp.int32, (8, FEAT), 0)
     pick_sum = (rows8 < 4).astype(F32).astype(BF16)
@@ -174,6 +184,47 @@
         z_in[i].wait_recv()
         offer(OTHER, i)
 
+    def hop(way, c):
+        return pltpu.make_async_remote_copy(
+            src_ref=wo_far.at[8 * way + 2 * at["x"] + c],
+            dst_ref=wo_far.at[8 * way + 2 * at["x"] + c],
+            send_sem=chain_send.at[way, c],
+            recv_sem=chain_recv.at[way, c],
+            device_id=z_next if way else z_prev,
+            device_id_type=MESH,
+        )
+
+    place = [lax.rem(4 - at["zl"], 4), lax.rem(at["zl"] + 1, 4)]
+
+    def chain(k):
+        for way in (0, 1):
+            if k < 2:
+
+                @pl.when(place[way] == 0)
+                def _():
+                    block = 8 * way + 2 * at["x"] + k
+                    first = (far["zh"] * 4 + lax.div(block, 4)) * FEAT
+                    pltpu.make_async_remote_copy(
+                        src_ref=wo_ref.at[pl.ds(lax.rem(block, 4) * HD, HD), pl.ds(first, FEAT)],
+                        dst_ref=wo_far.at[block],
+                        send_sem=chain_send.at[way, k],
+                        recv_sem=chain_recv.at[way, k],
+                        device_id=z_next if way else z_prev,
+                        device_id_type=MESH,
+                    ).start()
+
+            for n in (1, 2, 3):
+                c = k - 2 * n
+                if 0 <= c < 2:
+
+                    @pl.when(place[way] == n)
+                    def _():
+                        hop(way, c).wait_recv()
+                        hop(way, c).start()
+
+
+    chain(0)
+    chain(1)
     for s in st:
         s.wait_recv()
     compact = compact + stats[1] + stats[2] + stats[3]
@@ -239,9 +290,8 @@
 
     wo_loads = []
     y_dest = [at["y"], y_right["y"], y_left["y"], y_opp["y"]]
-    for b in range(8):
-        zh = at["zh"] if b < 4 else far["zh"]
-        first = (zh * 4 + y_dest[b % 4]) * FEAT
+    for b in range(4):
+        first = (at["zh"] * 4 + y_dest[b]) * FEAT
         for d in range(4):
             wo_loads.append(
                 load(
@@ -252,17 +302,7 @@
 
     offer_far(3)
     relay(OTHER, 2)
-    normalize(4)
-    relay(OTHER, 3)
-    for i in (1, 3):
-        from_left[OTHER][i].wait_recv()
-    normalize(5)
     weights_in(2)
-    for k in range(3):
-        project(2, k)
-    for i in (0, 2):
-        from_right[OTHER][i].wait_recv()
-    normalize(6)
     weights_in(3)
 
     def kv_part(side, core, d, p):
@@ -294,15 +334,32 @@
         spread_own(d, p)
 
     for p in (0, 1):
-        for i in (2 * p, 2 * p + 1):
+        groups = (2 * p, 2 * p + 1)
+        half_p = slice(p * HALF, (p + 1) * HALF)
+        normalize(4, groups)
+        from_left[OTHER][2 * p + 1].wait_recv()
+        normalize(5, groups)
+        for k in range(3):
+            project(2, k, half_p)
+        if p == 1:
+            chain(4)
+        from_right[OTHER][2 * p].wait_recv()
+        normalize(6, groups)
+        for i in groups:
             from_opp[OTHER][i].wait_recv()
-        normalize(7, (2 * p, 2 * p + 1))
+        normalize(7, groups)
+        if p == 0:
+            chain(2)
+            relay(OTHER, 3)
+            chain(3)
+        else:
+            chain(5)
         keep_p = pl.ds(p * HALF + at["row"] * QUARTER, QUARTER)
         give_p = pl.ds(p * HALF + mate["row"] * QUARTER, QUARTER)
         rows_p = pl.ds(p * QUARTER, QUARTER)
         halves = {}
         for k in (1, 2, 0):
-            project(3, k, slice(p * HALF, (p + 1) * HALF))
+            project(3, k, half_p)
             halves[k] = send(acc.at[k, give_p], arrived.at[p, k], mate)
         for k in (1, 2, 0):
             halves[k].wait_recv()
@@ -335,10 +392,12 @@
     z_arrived(2, 1)
     pass_on(2, 0)
     z_arrived(3, 1)
+    chain(6)
     pass_on(3, 0)
     for p in (0, 1):
         for d in (1, 2, 3):
             z_q[d, p].wait_recv()
+    chain(7)
 
     ones = jnp.ones((KEYS, HD), BF16)
     n_q = 4 * HALF
@@ -395,65 +454,85 @@
     mates_in(0)
     attend([(0, 1)], 0, n_q, False)
     pass_on(3, 1)
+    for way in (0, 1):
+
+        @pl.when(place[way] == 0)
+        def _():
+            for c in range(2):
+                hop(way, c).wait_recv()
+
+    def quarter(way, device):
+        return wo_far.at[pl.ds(8 * way + 2 * device["x"], 2)]
+
+    wo_left = [send(quarter(way, at), quarter(way, at), x_right) for way in (0, 1)]
+    wo_right = [send(quarter(way, at), quarter(way, at), x_left) for way in (1, 0)][::-1]
     attend([(1, 0), (2, 0)], 0, n_q, False)
+    for side in (1, 2):
+        mates_in(side)
+    attend([(1, 1), (2, 1)], 0, n_q, False)
     for d in range(4):
         for p in (0, 1):
             opp_in[d, p].wait_recv()
             to_mate(3, d, p)
-    for side in (1, 2, 3):
-        mates_in(side)
-
-    c_in = {}
+    mates_in(3)
+
+    c_in, f_in = {}, {}
     for begin in (2 * HALF, 0):
-        attend([(1, 1), (2, 1), (3, 0), (3, 1)], begin, 2 * HALF, False)
+        attend([(3, 0), (3, 1)], begin, 2 * HALF, False)
         for d in (begin // HALF + 1, begin // HALF):
             rows_d = slice(d * HALF, (d + 1) * HALF)
             value = (blended[rows_d, :HD] / blended[rows_d, HD:]).astype(BF16)
+            ctx_out[d] = value
+            f_in[d] = send(ctx_out.at[d], ctx.at[1, 0, d], far_back[d])
             if d == 0:
-                ctx[0, 0] = value
+                ctx[0, 0, 0] = value
             else:
-                ctx_out[d - 1] = value
-                c_in[d] = send(ctx_out.at[d - 1], ctx.at[0, d], z_back[d])
-    m_in = [send(ctx.at[0, 0], ctx.at[1, 0], mate)]
+                c_in[d] = send(ctx_out.at[d], ctx.at[0, 0, d], z_back[d])
+    wo_left[0].wait_recv()
+    wo_opp = [send(quarter(0, x_left), quarter(0, x_left), x_right)]
+    wo_right[1].wait_recv()
+    wo_opp.append(send(quarter(1, x_right), quarter(1, x_right), x_left))
+    m_in = [send(ctx.at[0, 0, 0], ctx.at[0, 1, 0], mate)]
     for d in (3, 2, 1):
         c_in[d].wait_recv()
-        m_in.append(send(ctx.at[0, d], ctx.at[1, d], mate))
+        m_in.append(send(ctx.at[0, 0, d], ctx.at[0, 1, d], mate))
+    for d in (3, 2, 1, 0):
+        f_in[d].wait_recv()
+        m_in.append(send(ctx.at[1, 0, d], ctx.at[1, 1, d], mate))
     for c in wo_loads:
         c.wait()
-
-    def product(z, y, j):
-        a = jnp.concatenate([ctx[j, d] for d in range(4)], axis=1)
-        return dot(a, wo_vm[4 * z + y])
+    for c in (wo_left[1], wo_right[0], *wo_opp):
+        c.wait_recv()
+    def product(y, j):
+        near = jnp.concatenate([ctx[0, j, d] for d in range(4)], axis=1)
+        away = jnp.concatenate([ctx[1, j, d] for d in range(4)], axis=1)
+        away_w = jnp.concatenate(
+            [wo_far[y_dest[y] * 4 + head_of[d]] for d in range(4)], axis=0
+        )
+        return dot(near, wo_vm[y]) + dot(away, away_w)
 
     out_in = {}
-    names = {}
 
     def push(name, j, value, device):
-        n = names.setdefault(name, len(names))
-        partial[n, j] = value.astype(BF16)
-        out_in[name, j] = send(partial.at[n, j], landed.at[n, j], device)
+        partial[name, j] = value.astype(BF16)
+        out_in[name, j] = send(partial.at[name, j], landed.at[name, j], device)
 
     def got(name, j):
         out_in[name, j].wait_recv()
-        return landed[names[name], j].astype(F32)
-
+        return landed[name, j].astype(F32)
+
+    push(OPP, 0, product(OPP, 0), y_right)
+    push(LEFT, 0, product(LEFT, 0), y_left)
+    for m in m_in:
+        m.wait_recv()
+    push(OPP, 1, product(OPP, 1), y_left)
+    push(RIGHT, 1, product(RIGHT, 1), y_right)
+    push(RIGHT, 0, product(RIGHT, 0) + got(OPP, 0), y_right)
+    push(LEFT, 1, product(LEFT, 1) + got(OPP, 1), y_left)
     for j in (0, 1):
-        if j == 1:
-            for m in m_in:
-                m.wait_recv()
-        push("o_opp", j, product(OTHER, OPP, j), y_right)
-        push("o_right", j, product(OTHER, LEFT, j), y_left)
-    for j in (0, 1):
-        push("w_opp", j, product(OWN, OPP, j), y_left)
-    for j in (0, 1):
-        push("o_left", j, product(OTHER, RIGHT, j) + got("o_opp", j), y_right)
-    for j in (0, 1):
-        push("w_left", j, product(OWN, RIGHT, j), y_right)
-    for j in (0, 1):
-        push("w_right", j, product(OWN, LEFT, j) + got("w_opp", j), y_left)
-        push("z", j, product(OTHER, HERE, j) + got("o_left", j) + got("o_right", j), far)
-    for j in (0, 1):
-        total = product(OWN, HERE, j) + got("w_left", j) + got("w_right", j) + got("z", j)
+        total = product(HERE, j)
+        order = (LEFT, RIGHT) if j == 0 else (RIGHT, LEFT)
+        total = total + got(order[0], j) + got(order[1], j)
         core = at["row"] if j == 0 else mate["row"]
         for p in (0, 1):
             first = p * HALF + core * QUARTER
@@ -462,23 +541,25 @@
             out_ref[pl.ds(first, QUARTER), :] = (piece + own).astype(BF16)
     for copy in copies:
         copy.wait_send()
+    for way in (0, 1):
+        for c in range(2):
+            hop(way, c).wait_send()
 
 
 def body(tokens, ln_gain, ln_bias, w_qkv, w_out):
-    gb = jnp.concatenate(
-        [jnp.broadcast_to(ln_gain[None], (8, FEAT)), jnp.broadcast_to(ln_bias[None], (8, FEAT))]
-    )
     any_spec = pl.BlockSpec(memory_space=pl.ANY)
+    vmem_spec = pl.BlockSpec(memory_space=pltpu.VMEM)
     return pl.pallas_call(
         kernel,
         out_shape=jax.ShapeDtypeStruct((TOK, FEAT), BF16),
-        in_specs=[any_spec] * 4,
+        in_specs=[any_spec, vmem_spec, vmem_spec, any_spec, any_spec],
         out_specs=pl.BlockSpec(memory_space=pltpu.VMEM),
         scratch_shapes=[
             pltpu.VMEM((8, TOK + GB, FEAT), BF16),
             pltpu.VMEM((TOK, 2 * FEAT), BF16),
             pltpu.VMEM((4, 3, 2 * FEAT, 4 * HD), BF16),
-            pltpu.VMEM((8, 4 * HD, FEAT), BF16),
+            pltpu.VMEM((4, 4 * HD, FEAT), BF16),
+            pltpu.VMEM((16, HD, FEAT), BF16),
             pltpu.VMEM((3, TOK, 4 * HD), F32),
             pltpu.VMEM((2, 3, QUARTER, 4 * HD), F32),
             pltpu.VMEM((8, 8, 128), F32),
@@ -488,18 +569,20 @@
             pltpu.VMEM((4, 2, 2, 4, HALF, HD), BF16),
             pltpu.VMEM((4 * HALF, 128), F32),
             pltpu.VMEM((4 * HALF, 2 * HD), F32),
-            pltpu.VMEM((3, HALF, HD), BF16),
-            pltpu.VMEM((2, 4, HALF, HD), BF16),
-            pltpu.VMEM((7, 2, HALF, FEAT), BF16),
-            pltpu.VMEM((7, 2, HALF, FEAT), BF16),
+            pltpu.VMEM((4, HALF, HD), BF16),
+            pltpu.VMEM((2, 2, 4, HALF, HD), BF16),
+            pltpu.VMEM((4, 2, HALF, FEAT), BF16),
+            pltpu.VMEM((4, 2, HALF, FEAT), BF16),
             pltpu.SemaphoreType.DMA((N_COPIES,)),
             pltpu.SemaphoreType.DMA((N_COPIES,)),
-            pltpu.SemaphoreType.DMA((66,)),
+            pltpu.SemaphoreType.DMA((49,)),
+            pltpu.SemaphoreType.DMA((2, 2)),
+            pltpu.SemaphoreType.DMA((2, 2)),
         ],
         compiler_params=pltpu.CompilerParams(
             collective_id=0, has_side_effects=True, vmem_limit_bytes=60 * 2**20
         ),
-    )(tokens, gb, w_qkv, w_out)
+    )(tokens, ln_gain[None], ln_bias[None], w_qkv, w_out)
 
 
 def solution(mesh):

time: 124 us -> 115 us (0.927)
  the two profiles are of different devices: /device:TPU:1 before, /device:TPU:64 now
where the time goes in v3:
time: 115 us
  Pallas kernels  111 us (97%)
  local copies, waits for them, and re-layouts  4.28 us (4%)
    pallas_call x1, Pallas kernels, body(): pl.pallas_call(kernel, out_shape=jax.ShapeDtypeStruct((TOK, FEAT), BF16),...  111 us

profile of v3, /device:TPU:64, one launch (start us, length us, event | category | flops | bytes accessed | tf_op | source)
XLA Modules:
  0.0 114.9 jit_solution(6419581774766217112)
XLA Ops:
  0.0 1.2 %broadcast_in_dim.6.gain_ref = bf16[1,384]{1,0:T(2,128)(2,1)} reshape(bf16[384]{0:T(512)(128)(2,1)} %param.6) | data formatting | bytes 1536 | tf_op jit(solution)/shard_map/broadcast_in_dim | solution.py:585
  1.2 1.3 %broadcast_in_dim.7.bias_ref = bf16[1,384]{1,0:T(2,128)(2,1)} reshape(bf16[384]{0:T(512)(128)(2,1)} %param.7) | data formatting | bytes 1536 | tf_op jit(solution)/shard_map/broadcast_in_dim | solution.py:585
  2.5 110.6 %shard_map.55 = bf16[512,384]{1,0:T(8,128)(2,1)} custom-call(bf16[512,384]{1,0:T(8,128)(2,1)} %tok_ref.1, bf16[1,384]{1,0:T(2,128)(2,1)} %broadcast_in_dim.6.gain_ref, bf16[1,384]{1,0:T(2,128)(2,1)} %broadcast_in_dim.7.bias_ref, bf16[3,3072,512]{2,1,0:T(8,128)(2,1)} %w_ref.1, bf16[512,3072]{1,0:T(8,128)(2,1)} %wo_ref.1), custom_call_target="tpu_custom_call" | custom-call | tf_op jit(solution)/shard_map/pallas_call | solution.py:552
  113.1 1.8 %copy.7 = bf16[512,384]{1,0:T(8,128)(2,1)} copy(bf16[512,384]{1,0:T(8,128)(2,1)} %shard_map.55) | data formatting | bytes 786432

commit v4 on v3

--- a/solution.py
+++ b/solution.py
@@ -23,7 +23,7 @@
 KEYS = 512
 OWN, OTHER = 0, 1
 HERE, RIGHT, LEFT, OPP = 0, 1, 2, 3
-N_COPIES = 140
+N_COPIES = 150
 
 
 def dot(a, b, dims=((1,), (0,))):
@@ -77,8 +77,6 @@
     z_fwd = [None] + [shifted(zl=d) for d in (1, 2, 3)]
     z_back = [None] + [shifted(zl=-d) for d in (1, 2, 3)]
     far_back = [shifted(zh=1, zl=-d) for d in range(4)]
-    z_prev = dict(at, zl=z_back[1]["zl"], zh=jnp.where(at["zl"] == 0, far["zh"], at["zh"]))
-    z_next = dict(at, zl=z_fwd[1]["zl"], zh=jnp.where(at["zl"] == 3, far["zh"], at["zh"]))
     copies = []
 
     def send(src, dst, device):
@@ -184,47 +182,70 @@
         z_in[i].wait_recv()
         offer(OTHER, i)
 
-    def hop(way, c):
+    def wo_copy(way, c, t, src, device):
         return pltpu.make_async_remote_copy(
-            src_ref=wo_far.at[8 * way + 2 * at["x"] + c],
+            src_ref=src,
             dst_ref=wo_far.at[8 * way + 2 * at["x"] + c],
-            send_sem=chain_send.at[way, c],
+            send_sem=chain_send.at[way, c, t],
             recv_sem=chain_recv.at[way, c],
-            device_id=z_next if way else z_prev,
+            device_id=device,
             device_id_type=MESH,
         )
 
-    place = [lax.rem(4 - at["zl"], 4), lax.rem(at["zl"] + 1, 4)]
-
-    def chain(k):
+    source = [at["zl"] == 0, at["zl"] == 3]
+    reached = [[dict(far, zl=jnp.int32(n)) for n in targets] for targets in ((3, 1), (0, 2))]
+    relays = [lax.rem(at["zl"], 2) == 1, lax.rem(at["zl"], 2) == 0]
+    beside = [z_back[1], z_fwd[1]]
+
+    def wo_relay_copy(way, c):
+        return wo_copy(way, c, 0, wo_far.at[8 * way + 2 * at["x"] + c], beside[way])
+
+    def wo_start():
         for way in (0, 1):
-            if k < 2:
-
-                @pl.when(place[way] == 0)
-                def _():
-                    block = 8 * way + 2 * at["x"] + k
+
+            @pl.when(source[way])
+            def _():
+                for c in (0, 1):
+                    block = 8 * way + 2 * at["x"] + c
                     first = (far["zh"] * 4 + lax.div(block, 4)) * FEAT
-                    pltpu.make_async_remote_copy(
-                        src_ref=wo_ref.at[pl.ds(lax.rem(block, 4) * HD, HD), pl.ds(first, FEAT)],
-                        dst_ref=wo_far.at[block],
-                        send_sem=chain_send.at[way, k],
-                        recv_sem=chain_recv.at[way, k],
-                        device_id=z_next if way else z_prev,
-                        device_id_type=MESH,
-                    ).start()
-
-            for n in (1, 2, 3):
-                c = k - 2 * n
-                if 0 <= c < 2:
-
-                    @pl.when(place[way] == n)
-                    def _():
-                        hop(way, c).wait_recv()
-                        hop(way, c).start()
-
-
-    chain(0)
-    chain(1)
+                    src = wo_ref.at[pl.ds(lax.rem(block, 4) * HD, HD), pl.ds(first, FEAT)]
+                    for n in (0, 1):
+                        wo_copy(way, c, n, src, reached[way][n]).start()
+
+    def wo_relay():
+        for way in (0, 1):
+
+            @pl.when(relays[way])
+            def _():
+                for c in (0, 1):
+                    wo_relay_copy(way, c).wait_recv()
+                    wo_relay_copy(way, c).start()
+
+    def wo_arrived():
+        for way in (0, 1):
+
+            @pl.when(jnp.logical_not(relays[way]))
+            def _():
+                for c in (0, 1):
+                    wo_relay_copy(way, c).wait_recv()
+
+    def wo_sent():
+        for way in (0, 1):
+
+            @pl.when(source[way])
+            def _():
+                for c in (0, 1):
+                    for n in (0, 1):
+                        wo_copy(
+                            way, c, n, wo_far.at[8 * way + 2 * at["x"] + c], reached[way][n]
+                        ).wait_send()
+
+            @pl.when(relays[way])
+            def _():
+                for c in (0, 1):
+                    wo_relay_copy(way, c).wait_send()
+
+    wo_start()
     for s in st:
         s.wait_recv()
     compact = compact + stats[1] + stats[2] + stats[3]
@@ -341,19 +362,13 @@
         normalize(5, groups)
         for k in range(3):
             project(2, k, half_p)
-        if p == 1:
-            chain(4)
         from_right[OTHER][2 * p].wait_recv()
         normalize(6, groups)
         for i in groups:
             from_opp[OTHER][i].wait_recv()
         normalize(7, groups)
         if p == 0:
-            chain(2)
             relay(OTHER, 3)
-            chain(3)
-        else:
-            chain(5)
         keep_p = pl.ds(p * HALF + at["row"] * QUARTER, QUARTER)
         give_p = pl.ds(p * HALF + mate["row"] * QUARTER, QUARTER)
         rows_p = pl.ds(p * QUARTER, QUARTER)
@@ -370,9 +385,9 @@
             for d in (1, 2, 3):
                 outgoing[p, d - 1, k] = whole[:, d * HD : (d + 1) * HD]
             if k == 0:
-                q_vm[0, rows_p] = whole[:, :HD]
+                q_vm[p, 0] = whole[:, :HD]
                 for d in (1, 2, 3):
-                    z_q[d, p] = send(outgoing.at[p, d - 1, 0], q_vm.at[d, rows_p], z_fwd[d])
+                    z_q[d, p] = send(outgoing.at[p, d - 1, 0], q_vm.at[p, d], z_fwd[d])
             else:
                 kv[0, 0, k - 1, 0, rows_p] = whole[:, :HD]
             if k == 2:
@@ -381,6 +396,7 @@
                         outgoing.at[p, d - 1, pl.ds(1, 2)], kv_part(0, 0, d, p), z_fwd[d]
                     )
                 spread_own(0, p)
+    wo_relay()
 
     z_arrived(1, 0)
     z_arrived(2, 0)
@@ -392,19 +408,17 @@
     z_arrived(2, 1)
     pass_on(2, 0)
     z_arrived(3, 1)
-    chain(6)
     pass_on(3, 0)
     for p in (0, 1):
         for d in (1, 2, 3):
             z_q[d, p].wait_recv()
-    chain(7)
 
     ones = jnp.ones((KEYS, HD), BF16)
     n_q = 4 * HALF
 
     def attend(slots, begin, size, first):
         at_q = pl.ds(begin, size)
-        q = q_vm[begin // HALF : (begin + size) // HALF].reshape(size, HD)
+        q = q_vm[begin // TOK : (begin + size) // TOK].reshape(size, HD)
         best = None if first else top[at_q, :]
         total = None if first else blended[at_q, :]
         steps = [(slot, i) for slot in slots for i in range(n_q // KEYS)]
@@ -454,12 +468,7 @@
     mates_in(0)
     attend([(0, 1)], 0, n_q, False)
     pass_on(3, 1)
-    for way in (0, 1):
-
-        @pl.when(place[way] == 0)
-        def _():
-            for c in range(2):
-                hop(way, c).wait_recv()
+    wo_arrived()
 
     def quarter(way, device):
         return wo_far.at[pl.ds(8 * way + 2 * device["x"], 2)]
@@ -477,35 +486,26 @@
     mates_in(3)
 
     c_in, f_in = {}, {}
-    for begin in (2 * HALF, 0):
-        attend([(3, 0), (3, 1)], begin, 2 * HALF, False)
-        for d in (begin // HALF + 1, begin // HALF):
-            rows_d = slice(d * HALF, (d + 1) * HALF)
+    for p in (0, 1):
+        attend([(3, 0), (3, 1)], p * TOK, TOK, False)
+        for d in (1, 2, 3, 0):
+            first = p * TOK + d * QUARTER
+            rows_d = slice(first, first + QUARTER)
             value = (blended[rows_d, :HD] / blended[rows_d, HD:]).astype(BF16)
-            ctx_out[d] = value
-            f_in[d] = send(ctx_out.at[d], ctx.at[1, 0, d], far_back[d])
+            ctx_out[p, d] = value
+            f_in[p, d] = send(ctx_out.at[p, d], ctx.at[1, 0, p, d], far_back[d])
             if d == 0:
-                ctx[0, 0, 0] = value
+                ctx[0, 0, p, 0] = value
             else:
-                c_in[d] = send(ctx_out.at[d], ctx.at[0, 0, d], z_back[d])
+                c_in[p, d] = send(ctx_out.at[p, d], ctx.at[0, 0, p, d], z_back[d])
     wo_left[0].wait_recv()
     wo_opp = [send(quarter(0, x_left), quarter(0, x_left), x_right)]
     wo_right[1].wait_recv()
     wo_opp.append(send(quarter(1, x_right), quarter(1, x_right), x_left))
-    m_in = [send(ctx.at[0, 0, 0], ctx.at[0, 1, 0], mate)]
-    for d in (3, 2, 1):
-        c_in[d].wait_recv()
-        m_in.append(send(ctx.at[0, 0, d], ctx.at[0, 1, d], mate))
-    for d in (3, 2, 1, 0):
-        f_in[d].wait_recv()
-        m_in.append(send(ctx.at[1, 0, d], ctx.at[1, 1, d], mate))
-    for c in wo_loads:
-        c.wait()
-    for c in (wo_left[1], wo_right[0], *wo_opp):
-        c.wait_recv()
-    def product(y, j):
-        near = jnp.concatenate([ctx[0, j, d] for d in range(4)], axis=1)
-        away = jnp.concatenate([ctx[1, j, d] for d in range(4)], axis=1)
+
+    def product(y, j, p):
+        near = jnp.concatenate([ctx[0, j, p, d] for d in range(4)], axis=1)
+        away = jnp.concatenate([ctx[1, j, p, d] for d in range(4)], axis=1)
         away_w = jnp.concatenate(
             [wo_far[y_dest[y] * 4 + head_of[d]] for d in range(4)], axis=0
         )
@@ -513,37 +513,47 @@
 
     out_in = {}
 
-    def push(name, j, value, device):
-        partial[name, j] = value.astype(BF16)
-        out_in[name, j] = send(partial.at[name, j], landed.at[name, j], device)
-
-    def got(name, j):
-        out_in[name, j].wait_recv()
-        return landed[name, j].astype(F32)
-
-    push(OPP, 0, product(OPP, 0), y_right)
-    push(LEFT, 0, product(LEFT, 0), y_left)
-    for m in m_in:
-        m.wait_recv()
-    push(OPP, 1, product(OPP, 1), y_left)
-    push(RIGHT, 1, product(RIGHT, 1), y_right)
-    push(RIGHT, 0, product(RIGHT, 0) + got(OPP, 0), y_right)
-    push(LEFT, 1, product(LEFT, 1) + got(OPP, 1), y_left)
-    for j in (0, 1):
-        total = product(HERE, j)
-        order = (LEFT, RIGHT) if j == 0 else (RIGHT, LEFT)
-        total = total + got(order[0], j) + got(order[1], j)
-        core = at["row"] if j == 0 else mate["row"]
-        for p in (0, 1):
+    def push(name, j, p, value, device):
+        partial[name, j, p] = value.astype(BF16)
+        out_in[name, j, p] = send(partial.at[name, j, p], landed.at[name, j, p], device)
+
+    def got(name, j, p):
+        out_in[name, j, p].wait_recv()
+        return landed[name, j, p].astype(F32)
+
+    for p in (0, 1):
+        m_in = []
+        for d in (1, 2, 3):
+            c_in[p, d].wait_recv()
+        m_in.append(send(ctx.at[0, 0, p], ctx.at[0, 1, p], mate))
+        for d in (1, 2, 3, 0):
+            f_in[p, d].wait_recv()
+        m_in.append(send(ctx.at[1, 0, p], ctx.at[1, 1, p], mate))
+        if p == 0:
+            for c in wo_loads:
+                c.wait()
+            for c in (wo_left[1], wo_right[0], *wo_opp):
+                c.wait_recv()
+        push(OPP, 0, p, product(OPP, 0, p), y_right)
+        push(LEFT, 0, p, product(LEFT, 0, p), y_left)
+        for m in m_in:
+            m.wait_recv()
+        push(OPP, 1, p, product(OPP, 1, p), y_left)
+        push(RIGHT, 1, p, product(RIGHT, 1, p), y_right)
+        push(RIGHT, 0, p, product(RIGHT, 0, p) + got(OPP, 0, p), y_right)
+        push(LEFT, 1, p, product(LEFT, 1, p) + got(OPP, 1, p), y_left)
+    for p in (0, 1):
+        for j in (0, 1):
+            total = product(HERE, j, p)
+            order = (LEFT, RIGHT) if j == 0 else (RIGHT, LEFT)
+            total = total + got(order[0], j, p) + got(order[1], j, p)
+            core = at["row"] if j == 0 else mate["row"]
             first = p * HALF + core * QUARTER
-            piece = total[p * QUARTER : (p + 1) * QUARTER]
             own = slabs[0, pl.ds(GB + first, QUARTER), :].astype(F32)
-            out_ref[pl.ds(first, QUARTER), :] = (piece + own).astype(BF16)
+            out_ref[pl.ds(first, QUARTER), :] = (total + own).astype(BF16)
     for copy in copies:
         copy.wait_send()
-    for way in (0, 1):
-        for c in range(2):
-            hop(way, c).wait_send()
+    wo_sent()
 
 
 def body(tokens, ln_gain, ln_bias, w_qkv, w_out):
@@ -565,18 +575,18 @@
             pltpu.VMEM((8, 8, 128), F32),
             pltpu.VMEM((128, 128), F32),
             pltpu.VMEM((2, 3, 3, QUARTER, HD), BF16),
-            pltpu.VMEM((4, HALF, HD), BF16),
+            pltpu.VMEM((2, 4, QUARTER, HD), BF16),
             pltpu.VMEM((4, 2, 2, 4, HALF, HD), BF16),
             pltpu.VMEM((4 * HALF, 128), F32),
             pltpu.VMEM((4 * HALF, 2 * HD), F32),
-            pltpu.VMEM((4, HALF, HD), BF16),
-            pltpu.VMEM((2, 2, 4, HALF, HD), BF16),
-            pltpu.VMEM((4, 2, HALF, FEAT), BF16),
-            pltpu.VMEM((4, 2, HALF, FEAT), BF16),
+            pltpu.VMEM((2, 4, QUARTER, HD), BF16),
+            pltpu.VMEM((2, 2, 2, 4, QUARTER, HD), BF16),
+            pltpu.VMEM((4, 2, 2, QUARTER, FEAT), BF16),
+            pltpu.VMEM((4, 2, 2, QUARTER, FEAT), BF16),
             pltpu.SemaphoreType.DMA((N_COPIES,)),
             pltpu.SemaphoreType.DMA((N_COPIES,)),
             pltpu.SemaphoreType.DMA((49,)),
-            pltpu.SemaphoreType.DMA((2, 2)),
+            pltpu.SemaphoreType.DMA((2, 2, 2)),
             pltpu.SemaphoreType.DMA((2, 2)),
         ],
         compiler_params=pltpu.CompilerParams(

time: 115 us -> 109 us (0.948)
  the two profiles are of different devices: /device:TPU:64 before, /device:TPU:1 now
where the time goes in v4:
time: 109 us; the launch traced here: 108 us
  Pallas kernels  104 us (95%)
  local copies, waits for them, and re-layouts  4.28 us (4%)
    pallas_call x1, Pallas kernels, body(): pl.pallas_call(kernel, out_shape=jax.ShapeDtypeStruct((TOK, FEAT), BF16),...  104 us

profile of v4, /device:TPU:1, one launch (start us, length us, event | category | flops | bytes accessed | tf_op | source)
XLA Modules:
  0.0 108.3 jit_solution(13297355322710820100)
XLA Ops:
  0.0 1.2 %broadcast_in_dim.6.gain_ref = bf16[1,384]{1,0:T(2,128)(2,1)} reshape(bf16[384]{0:T(512)(128)(2,1)} %param.6) | data formatting | bytes 1536 | tf_op jit(solution)/shard_map/broadcast_in_dim | solution.py:595
  1.2 1.3 %broadcast_in_dim.7.bias_ref = bf16[1,384]{1,0:T(2,128)(2,1)} reshape(bf16[384]{0:T(512)(128)(2,1)} %param.7) | data formatting | bytes 1536 | tf_op jit(solution)/shard_map/broadcast_in_dim | solution.py:595
  2.5 104.0 %shard_map.55 = bf16[512,384]{1,0:T(8,128)(2,1)} custom-call(bf16[512,384]{1,0:T(8,128)(2,1)} %tok_ref.1, bf16[1,384]{1,0:T(2,128)(2,1)} %broadcast_in_dim.6.gain_ref, bf16[1,384]{1,0:T(2,128)(2,1)} %broadcast_in_dim.7.bias_ref, bf16[3,3072,512]{2,1,0:T(8,128)(2,1)} %w_ref.1, bf16[512,3072]{1,0:T(8,128)(2,1)} %wo_ref.1), custom_call_target="tpu_custom_call" | custom-call | tf_op jit(solution)/shard_map/pallas_call | solution.py:562
  106.5 1.8 %copy.7 = bf16[512,384]{1,0:T(8,128)(2,1)} copy(bf16[512,384]{1,0:T(8,128)(2,1)} %shard_map.55) | data formatting | bytes 786432

commit v5 on v4

--- a/solution.py
+++ b/solution.py
@@ -32,8 +32,7 @@
 
 def kernel(
     tok_ref,
-    gain_ref,
-    bias_ref,
+    scales_ref,
     w_ref,
     wo_ref,
     out_ref,
@@ -104,8 +103,8 @@
     own_tok = load(tok_ref, slabs.at[0, pl.ds(GB, TOK)])
     slabs[0, :GB, :] = jnp.where(
         lax.broadcasted_iota(jnp.int32, (GB, FEAT), 0) < 8,
-        jnp.broadcast_to(gain_ref[...].astype(F32), (GB, FEAT)),
-        jnp.broadcast_to(bias_ref[...].astype(F32), (GB, FEAT)),
+        jnp.broadcast_to(scales_ref[0:1].astype(F32), (GB, FEAT)),
+        jnp.broadcast_to(scales_ref[1:2].astype(F32), (GB, FEAT)),
     ).astype(BF16)
 
     y_of = [at["y"], y_left["y"], y_right["y"], y_opp["y"]]
@@ -367,8 +366,6 @@
         for i in groups:
             from_opp[OTHER][i].wait_recv()
         normalize(7, groups)
-        if p == 0:
-            relay(OTHER, 3)
         keep_p = pl.ds(p * HALF + at["row"] * QUARTER, QUARTER)
         give_p = pl.ds(p * HALF + mate["row"] * QUARTER, QUARTER)
         rows_p = pl.ds(p * QUARTER, QUARTER)
@@ -376,6 +373,8 @@
         for k in (1, 2, 0):
             project(3, k, half_p)
             halves[k] = send(acc.at[k, give_p], arrived.at[p, k], mate)
+        if p == 0:
+            relay(OTHER, 3)
         for k in (1, 2, 0):
             halves[k].wait_recv()
             whole = acc[k, keep_p, :] + arrived[p, k]
@@ -562,7 +561,7 @@
     return pl.pallas_call(
         kernel,
         out_shape=jax.ShapeDtypeStruct((TOK, FEAT), BF16),
-        in_specs=[any_spec, vmem_spec, vmem_spec, any_spec, any_spec],
+        in_specs=[any_spec, vmem_spec, any_spec, any_spec],
         out_specs=pl.BlockSpec(memory_space=pltpu.VMEM),
         scratch_shapes=[
             pltpu.VMEM((8, TOK + GB, FEAT), BF16),
@@ -592,7 +591,7 @@
         compiler_params=pltpu.CompilerParams(
             collective_id=0, has_side_effects=True, vmem_limit_bytes=60 * 2**20
         ),
-    )(tokens, ln_gain[None], ln_bias[None], w_qkv, w_out)
+    )(tokens, jnp.stack([ln_gain, ln_bias]), w_qkv, w_out)
 
 
 def solution(mesh):

time: 109 us -> 109 us (level)
  local copies, waits for them, and re-layouts: 4.28 us -> 3.14 us
    broadcast_in_dim x2 -> x0, local copies, waits for them, and re-layouts: 2.5 us -> none  [the longest x1 1.25 us: body(): ln_bias[None]]
    another operation x0 -> x2, local copies, waits for them, and re-layouts: none -> 1.36 us  [body(): jnp.stack([ln_gain, ln_bias])]
where the time goes in v5:
time: 109 us; the launch traced here: 108 us
  Pallas kernels  105 us (96%)
  local copies, waits for them, and re-layouts  3.14 us (3%)
    pallas_call x1, Pallas kernels, body(): pl.pallas_call(kernel, out_shape=jax.ShapeDtypeStruct((TOK, FEAT), BF16),...  105 us

profile of v5, /device:TPU:1, one launch (start us, length us, event | category | flops | bytes accessed | tf_op | source)
XLA Modules:
  0.0 108.5 jit_solution(6218454295265836669)
XLA Ops:
  0.0 0.7 stack.9
  0.7 0.7 stack.10
  1.4 0.6 pad_maximum_fusion.scales_ref
  1.9 104.7 %shard_map.55 = bf16[512,384]{1,0:T(8,128)(2,1)} custom-call(bf16[512,384]{1,0:T(8,128)(2,1)} %tok_ref.1, bf16[2,384]{1,0:T(2,128)(2,1)} %pad_maximum_fusion.scales_ref, bf16[3,3072,512]{2,1,0:T(8,128)(2,1)} %w_ref.1, bf16[512,3072]{1,0:T(8,128)(2,1)} %wo_ref.1), custom_call_target="tpu_custom_call" | custom-call | tf_op jit(solution)/shard_map/pallas_call | solution.py:561
  106.7 1.8 %copy.7 = bf16[512,384]{1,0:T(8,128)(2,1)} copy(bf16[512,384]{1,0:T(8,128)(2,1)} %shard_map.55) | data formatting | bytes 786432
